TPU v7x, 32 devices: a whole 2x2x4 slice. The times are simulated.
32 devices in a mesh: blk: 8 (over y, x, core), tp: 4 (over z).
Axes of the slice: x: 2, y: 2, z: 4, core: 2. Of those that a mesh axis runs over, the one named last changes fastest.
Arguments:
- mantissa: bfloat16 [8, 2880, 2880], P('blk', 'tp'), may hold values from -6 to 6
- exponent: int32 [8, 2880, 90], P('blk', 'tp'), may hold values from -3 to 1
- home: int32 [8], replicated, may hold values from 0 to 7, as said below
- queries: bfloat16 [32, 4096], P('blk', 'tp'), may hold values from -8 to 8
- keys: bfloat16 [32, 2048, 512], P('blk', None, 'tp'), may hold values from -8 to 8
- values: bfloat16 [32, 2048, 512], P('blk', None, 'tp'), may hold values from -6 to 6
- lengths: int32 [32], P('blk'), may hold values from 2 to 2048
Outputs:
- served: bfloat16 [8, 2880, 2880], P('blk', 'tp')
- checks: float32 [8, 2880, 90], P('blk', 'tp')
- energy: float32 [8], P('blk')
- attended: bfloat16 [32, 4096], P('blk', 'tp')
Inputs may be any that keep to these rules, and one draw needn't show every extreme that they name: home[e] = (e + r) mod 8 for one whole number r of 1 to 3, the same for every expert.
All inputs are finite; a program needn't handle non-finite values.
Results may differ from a plain program's by a relative error of at most 0.0095.
Values may be sent and summed in bfloat16 or wider, within the bound.
No kernel may reach another device: no remote copies, remote signals or barrier semaphores. Data moves between devices by JAX's collectives and lax.ppermute only.
A program may use at most 64 MiB of HBM per device.

v0:
```python
import jax
import jax.numpy as jnp
from jax import lax
from jax.sharding import PartitionSpec as P

D = 2880
F = 2880
QUERY_HEADS = 64
KEY_VALUE_HEADS = 8
HEAD_SIZE = 64


def from_behind(value, axis, steps):
    count = lax.axis_size(axis)
    pairs = [(source, (source + steps) % count) for source in range(count)]
    return lax.ppermute(value, axis, pairs)


def local(mantissa, exponent, home, queries, keys, values, lengths):
    rows = mantissa.shape[1]
    width = mantissa.shape[2]
    blocks = exponent.shape[2]
    scale = jnp.exp2(exponent[0].astype(jnp.float32))
    fresh = (
        mantissa[0].astype(jnp.float32).reshape(rows, blocks, width // blocks) * scale[:, :, None]
    )
    fresh = fresh.reshape(rows, width).astype(jnp.bfloat16)
    distance = home[0]

    def single_step(index, carry):
        return from_behind(carry, "blk", 1)

    def double_step(index, carry):
        return from_behind(carry, "blk", 2)

    served = lax.fori_loop(0, distance // 2, double_step, fresh)
    served = lax.fori_loop(0, distance % 2, single_step, served)
    wide = served.astype(jnp.float32)
    checks = jnp.sum(wide.reshape(rows, blocks, width // blocks), axis=2)
    energy = lax.psum(jnp.sum(wide * wide), "tp") / (F * D)
    seqs = queries.shape[0]
    slots_len = keys.shape[1]
    kv_heads = keys.shape[2] // HEAD_SIZE
    query_groups = QUERY_HEADS // KEY_VALUE_HEADS
    query_input = queries.reshape(seqs, kv_heads, query_groups, HEAD_SIZE)
    key_cache = keys.reshape(seqs, slots_len, kv_heads, HEAD_SIZE)
    value_cache = values.reshape(seqs, slots_len, kv_heads, HEAD_SIZE)
    scores = jnp.einsum(
        "bgrh,blgh->bgrl", query_input, key_cache, preferred_element_type=jnp.float32
    ) * HEAD_SIZE ** (-0.5)
    live = jnp.arange(slots_len, dtype=jnp.int32)[None, :] < lengths[:, None]
    scores = jnp.where(live[:, None, None, :], scores, jnp.float32(-1e30))
    top = jnp.max(scores, axis=3, keepdims=True)
    expd = jnp.exp(scores - top)
    total = jnp.sum(expd, axis=3, keepdims=True)
    probs = (expd / total).astype(jnp.bfloat16)
    mixed = jnp.einsum("bgrl,blgh->bgrh", probs, value_cache, preferred_element_type=jnp.float32)
    attended = mixed.astype(jnp.bfloat16).reshape(seqs, kv_heads * query_groups * HEAD_SIZE)
    return (served[None], checks[None], energy.reshape(1), attended)


def solution(mesh):
    placed = (
        P("blk", "tp", None),
        P("blk", "tp", None),
        P(),
        P("blk", "tp"),
        P("blk", None, "tp"),
        P("blk", None, "tp"),
        P("blk"),
    )
    return jax.shard_map(
        local,
        mesh=mesh,
        in_specs=placed,
        out_specs=(P("blk", "tp", None), P("blk", "tp", None), P("blk"), P("blk", "tp")),
        check_vma=False,
    )
```

profile of v0, /device:TPU:0, one launch (start us, length us, event | category | flops | bytes accessed | tf_op | source)
XLA Modules:
  0.0 217.4 jit_solution(419405699716802344)
XLA Ops:
  3.2 0.7 iota_compare_fusion
  4.0 0.8 reshape.65
  4.8 1.3 multiply_exponential_fusion
  6.1 2.9 %copy.17 = bf16[4,2048,128]{1,2,0:T(8,128)(2,1)S(1)} copy(bf16[4,2048,128]{2,1,0:T(8,128)(2,1)} %param.15) | data formatting | bytes 4194304 | tf_op args[4]
  9.1 0.4 fusion.4
  9.5 0.3 fusion.6
  9.7 2.9 %copy.18 = bf16[4,2048,128]{1,2,0:T(8,128)(2,1)S(1)} copy(bf16[4,2048,128]{2,1,0:T(8,128)(2,1)} %param.16) | data formatting | bytes 4194304 | tf_op args[5]
  12.7 0.7 convolution_convert_fusion
  13.4 0.7 reshape.68
  14.1 6.5 %copy.14 = bf16[1,720,2880]{1,2,0:T(8,128)(2,1)} copy(bf16[1,720,2880]{2,1,0:T(8,128)(2,1)} %param.11) | data formatting | bytes 8294400 | tf_op args[0]
  20.6 5.1 %fusion.1 = bf16[720,2880]{0,1:T(8,128)(2,1)} fusion(bf16[1,720,2880]{1,2,0:T(8,128)(2,1)} %copy.14, f32[720,90]{0,1:T(8,128)S(1)} %bitcast.29), kind=kLoop, calls=%fused_computation.2 | loop fusion | flops 6220800 | bytes 8553600 | tf_op jit(solution)/shard_map/convert_element_type | solution.py:27
  25.7 6.4 %copy.15 = bf16[720,2880]{1,0:T(8,128)(2,1)} copy(bf16[720,2880]{0,1:T(8,128)(2,1)} %fusion.1) | data formatting | bytes 8294400 | tf_op jit(solution)/shard_map/while | solution.py:36
  32.1 100.3 %while.20 = (s32[]{:T(128)}, bf16[720,2880]{1,0:T(8,128)(2,1)}, s32[]{:T(128)}, s32[]{:T(128)}) while((s32[]{:T(128)}, bf16[720,2880]{1,0:T(8,128)(2,1)}, s32[]{:T(128)}, s32[]{:T(128)}) %tuple.36), condition=%wide.region_1.2_spmd, body=%wide.region_0.1_spmd.sunk | while | flops 2 | bytes 24883292 | solution.py:36
  32.1 3.0 %collective-permute-start = (bf16[720,2880]{1,0:T(8,128)(2,1)}, bf16[720,2880]{1,0:T(8,128)(2,1)}, u32[]{:S(2)}, u32[]{:S(2)}) collective-permute-start(bf16[720,2880]{1,0:T(8,128)(2,1)} %get-tuple-element.102), channel_id=1, source_target_pairs={{0,8},{4,12},{8,16},{12,20},{16,24},{20,28},{24,0},{28,4},{1,9},{5... | collective-permute-start | bytes 12441608 | tf_op jit(solution)/shard_map/while/body/ppermute | solution.py:16
  35.1 92.8 %collective-permute-done = bf16[720,2880]{1,0:T(8,128)(2,1)} collective-permute-done((bf16[720,2880]{1,0:T(8,128)(2,1)}, bf16[720,2880]{1,0:T(8,128)(2,1)}, u32[]{:S(2)}, u32[]{:S(2)}) %collective-permute-start) | collective-permute-done | bytes 4147232 | tf_op jit(solution)/shard_map/while/body/ppermute | solution.py:16
  127.9 4.5 %copy.27 = bf16[720,2880]{1,0:T(8,128)(2,1)} copy(bf16[720,2880]{1,0:T(8,128)(2,1)} %collective-permute-done) | data formatting | bytes 8294400 | tf_op jit(solution)/shard_map/while
  132.4 54.1 %while.21 = (s32[]{:T(128)}, bf16[720,2880]{1,0:T(8,128)(2,1)}, s32[]{:T(128)}, s32[]{:T(128)}) while((s32[]{:T(128)}, bf16[720,2880]{1,0:T(8,128)(2,1)}, s32[]{:T(128)}, s32[]{:T(128)}) %tuple.39), condition=%wide.region_3.4_spmd, body=%wide.region_2.3_spmd.sunk | while | flops 2 | bytes 24883292 | solution.py:37
  132.4 0.0 collective-permute-start.1
  132.4 49.6 %collective-permute-done.1 = bf16[720,2880]{1,0:T(8,128)(2,1)} collective-permute-done((bf16[720,2880]{1,0:T(8,128)(2,1)}, bf16[720,2880]{1,0:T(8,128)(2,1)}, u32[]{:S(2)}, u32[]{:S(2)}) %collective-permute-start.1) | collective-permute-done | bytes 4147232 | tf_op jit(solution)/shard_map/while/body/ppermute | solution.py:16
  182.0 4.5 %copy.33 = bf16[720,2880]{1,0:T(8,128)(2,1)} copy(bf16[720,2880]{1,0:T(8,128)(2,1)} %collective-permute-done.1) | data formatting | bytes 8294400 | tf_op jit(solution)/shard_map/while
  186.6 6.5 %copy.16 = bf16[720,2880]{0,1:T(8,128)(2,1)} copy(bf16[720,2880]{1,0:T(8,128)(2,1)} %get-tuple-element.41) | data formatting | bytes 8294400 | tf_op jit(solution)/shard_map/while | solution.py:37
  193.1 5.1 %multiply_reduce_fusion = f32[]{:T(128)} fusion(bf16[720,2880]{0,1:T(8,128)(2,1)} %copy.16), kind=kLoop, calls=%fused_computation.3 | loop fusion | flops 6220799 | bytes 4147204 | tf_op jit(solution)/shard_map/reduce_sum | solution.py:40
  198.2 12.8 %psum.7 = f32[]{:T(128)} all-reduce(f32[]{:T(128)} %multiply_reduce_fusion), channel_id=1, replica_groups=mesh['blk'=8,'tp'=4] {'tp'}, use_global_device_ids=true, to_apply=%region_6.7 | all-reduce | flops 1 | bytes 8 | tf_op jit(solution)/shard_map/psum | solution.py:40
  211.6 3.8 %reduce_sum.27 = f32[720,90]{0,1:T(8,128)S(1)} reduce(bf16[720,90,32]{0,2,1:T(8,128)(2,1)} %bitcast.25, f32[]{:T(128)} %constant.37.clone.1), dimensions={2}, to_apply=%region_4.5 | reduce | flops 2008800 | bytes 4406404 | tf_op jit(solution)/shard_map/reduce_sum | solution.py:39
  215.4 0.9 broadcast_in_dim.25
  (1 shorter events, 0.0 us)
Async XLA Ops:
  32.1 95.8 %collective-permute-start = (bf16[720,2880]{1,0:T(8,128)(2,1)}, bf16[720,2880]{1,0:T(8,128)(2,1)}, u32[]{:S(2)}, u32[]{:S(2)}) collective-permute-start(bf16[720,2880]{1,0:T(8,128)(2,1)} %get-tuple-element.102), channel_id=1, source_target_pairs={{0,8},{4,12},{8,16},{12,20},{16,24},{20,28},{24,0},{28,4},{1,9},{5... | collective-permute-start | bytes 12441608 | tf_op jit(solution)/shard_map/while/body/ppermute | solution.py:16
  132.4 49.6 %collective-permute-start.1 = (bf16[720,2880]{1,0:T(8,128)(2,1)}, bf16[720,2880]{1,0:T(8,128)(2,1)}, u32[]{:S(2)}, u32[]{:S(2)}) collective-permute-start(bf16[720,2880]{1,0:T(8,128)(2,1)} %get-tuple-element.114), channel_id=1, source_target_pairs={{0,4},{4,8},{8,12},{12,16},{16,20},{20,24},{24,28},{28,0},{1,5},{5... | collective-permute-start | bytes 12441608 | tf_op jit(solution)/shard_map/while/body/ppermute | solution.py:16
where the time goes:
time: 218 us; the launch traced here: 217 us
  waiting for transfers between devices  142 us (65%)
  local copies, waits for them, and re-layouts  36.7 us (17%)
  other arithmetic  16.3 us (7%)
  blocking collectives  12.8 us (6%)
  between operations  5.06 us (2%)
  starting transfers between devices  2.97 us (1%)
    ppermute x2, waiting for transfers between devices, from_behind(): return lax.ppermute(value, axis, pairs)  142 us
    psum x1, blocking collectives, local(): energy = lax.psum(jnp.sum(wide * wide), 'tp') / (F * D)  12.8 us
    unnamed x4, local copies, waits for them, and re-layouts  12.4 us
    while x2, local copies, waits for them, and re-layouts  9.04 us
    while x1, local copies, waits for them, and re-layouts, local(): served = lax.fori_loop(0, distance % 2, single_step, served)  6.51 us
    while x1, local copies, waits for them, and re-layouts, local(): served = lax.fori_loop(0, distance // 2, double_step, fresh)  6.41 us
    reduce_sum x1, other arithmetic, local(): energy = lax.psum(jnp.sum(wide * wide), 'tp') / (F * D)  5.13 us
    convert_element_type x1, other arithmetic, local(): fresh = fresh.reshape(rows, width).astype(jnp.bfloat16)  5.1 us
  transfers between devices with their start and end apart: 2, of which 2 were waited for; matrix products, arithmetic and copies ran while one was open for 0% of the time, Pallas kernels for 0%

commit v1 on v0

v1 whole, which is shorter than its diff:
```python
import functools

import jax
import jax.numpy as jnp
from jax import lax
from jax.experimental import pallas as pl
from jax.experimental.pallas import tpu as pltpu
from jax.sharding import PartitionSpec as P


HEAD_SIZE = 64
LARGEST_DISTANCE = 3
LANES = 128
SUBLANES = 16
FIRST = 112
HBM = pl.BlockSpec(memory_space=pltpu.HBM)
VMEM = pl.BlockSpec(memory_space=pltpu.VMEM)
SMEM = pl.BlockSpec(memory_space=pltpu.SMEM)
PARAMS = pltpu.CompilerParams(vmem_limit_bytes=16 * 2**20)


def tiles(first, last):
    marks = [first] + [mark for mark in range(0, last, LANES) if mark > first] + [last]
    return list(zip(marks[:-1], marks[1:]))


def membership(blocks, width):
    block = width // blocks
    offset = lax.broadcasted_iota(jnp.int32, (blocks, width), 1) - block * lax.broadcasted_iota(
        jnp.int32, (blocks, width), 0
    )
    return jnp.where((offset >= 0) & (offset < block), 1.0, 0.0).astype(jnp.bfloat16)


def packing(rows, width):
    columns, left = divmod(width, LANES)
    beside = LANES // left if left and LANES % left == 0 else 1
    group = -(-rows // (beside * SUBLANES)) * SUBLANES if left else 0
    return columns, left, min(group, rows), columns * rows + group


def packed_rows(first, last, width):
    return sum(packing(b - a, width)[3] for a, b in tiles(first, last))


def pack(narrow, out_buf, at):
    rows, width = narrow.shape
    columns, left, group, _ = packing(rows, width)
    for column in range(columns):
        out_buf[pl.ds(at + column * rows, rows)] = narrow[:, column * LANES : (column + 1) * LANES]
    for g, row in enumerate(range(0, rows, group) if left else ()):
        height = min(group, rows - row)
        out_buf[pl.ds(at + columns * rows, height), g * left : (g + 1) * left] = narrow[
            row : row + height, columns * LANES :
        ]


def unpack(packed, at, buf, first, rows):
    columns, left, group, _ = packing(rows, buf.shape[1])
    for column in range(columns):
        buf[pl.ds(first, rows), column * LANES : (column + 1) * LANES] = packed[pl.ds(at + column * rows, rows)]
    for g, row in enumerate(range(0, rows, group) if left else ()):
        height = min(group, rows - row)
        buf[pl.ds(first + row, height), columns * LANES :] = packed[
            pl.ds(at + columns * rows, height), g * left : (g + 1) * left
        ]


def scales(expo_ref, a, b):
    return jnp.exp2(expo_ref[:, 0, a:b].astype(jnp.float32)).astype(jnp.bfloat16)


def spread(scale, member):
    return lax.dot_general(scale, member, (((0,), (0,)), ((), ())), preferred_element_type=jnp.float32)


def sum_blocks(member, served):
    return lax.dot_general(member, served, (((1,), (1,)), ((), ())), preferred_element_type=jnp.float32)


def dequantize_kernel(chunks, scaled, counted, mant_hbm, expo_ref, before_ref, *refs):
    fresh_hbms, refs = refs[: len(chunks)], refs[len(chunks) :]
    power_ref, mant_buf, out_buf, in_sem, out_sem, scale_sem = refs
    blocks, width = expo_ref.shape[0], mant_hbm.shape[1]
    spans = [(k, a, b) for k, chunk in enumerate(chunks) for a, b in tiles(*chunk)]
    spans += [(None, a, b) for chunk in counted for a, b in tiles(*chunk)]
    loads, stores = [], []
    into = 0
    for n, (_, a, b) in enumerate(spans):
        load = pltpu.make_async_copy(
            mant_hbm.at[pl.ds(a, b - a)], mant_buf.at[pl.ds(into, b - a)], in_sem.at[n]
        )
        load.start()
        loads.append(load)
        into += b - a
    member = membership(blocks, width)
    power = jnp.zeros((SUBLANES, width), jnp.float32)
    at, into = 0, 0
    start = dict.fromkeys(range(len(chunks)), 0)
    if scaled:
        size = -(-blocks // SUBLANES) * SUBLANES
        end = out_buf.shape[0] - size
        out_buf[pl.ds(end, blocks), : scaled[1] - scaled[0]] = scales(expo_ref, *scaled)
        store = pltpu.make_async_copy(
            out_buf.at[pl.ds(end, size)], fresh_hbms[0].at[pl.ds(fresh_hbms[0].shape[0] - size, size)], scale_sem
        )
        store.start()
        stores.append(store)
    for n, (k, a, b) in enumerate(spans):
        rows = b - a
        wide = spread(scales(expo_ref, a, b), member)
        loads[n].wait()
        wide = mant_buf[pl.ds(into, rows)].astype(jnp.float32) * wide
        into += rows
        if k is not None:
            size = packing(rows, width)[3]
            pack(wide.astype(jnp.bfloat16), out_buf, at)
            store = pltpu.make_async_copy(
                out_buf.at[pl.ds(at, size)], fresh_hbms[k].at[pl.ds(start[k], size)], out_sem.at[n]
            )
            store.start()
            stores.append(store)
            at += size
            start[k] += size
        for row in range(0, rows, SUBLANES):
            power = power + wide[row : row + SUBLANES] * wide[row : row + SUBLANES]
    power_ref[0] = before_ref[0] + jnp.sum(power)
    for store in stores:
        store.wait()


def dequantize(mant, expo, before, chunks, sizes, scaled=None, counted=()):
    width = mant.shape[1]
    every = list(chunks) + list(counted)
    count = sum(len(tiles(*chunk)) for chunk in every)
    *fresh, power = pl.pallas_call(
        functools.partial(dequantize_kernel, chunks, scaled, counted),
        out_shape=tuple(jax.ShapeDtypeStruct((size, LANES), jnp.bfloat16) for size in sizes)
        + (jax.ShapeDtypeStruct((1,), jnp.float32),),
        in_specs=[HBM, VMEM, SMEM],
        out_specs=(HBM,) * len(chunks) + (SMEM,),
        scratch_shapes=[
            pltpu.VMEM((sum(b - a for a, b in every), width), jnp.bfloat16),
            pltpu.VMEM((sum(sizes), LANES), jnp.bfloat16),
            pltpu.SemaphoreType.DMA((count,)),
            pltpu.SemaphoreType.DMA((count,)),
            pltpu.SemaphoreType.DMA,
        ],
        compiler_params=PARAMS,
    )(mant, expo, before)
    return fresh, power


def attach_kernel(at, divisor, count, me_ref, *refs):
    power_refs, (_, out_hbm, buf, sem) = refs[:count], refs[count:]
    total = jnp.float32(0)
    for device in range(count):
        behind = lax.rem(me_ref[0] - device + count, count)
        one = power_refs[0][0]
        for n in range(1, count):
            one = jnp.where(behind == n, power_refs[n][0], one)
        total = total + one
    rest = jnp.full(buf.shape, total, jnp.float32) / divisor
    row = lax.broadcasted_iota(jnp.int32, buf.shape, 0)
    pieces = jnp.zeros(buf.shape, jnp.float32)
    for n in range(3):
        piece = rest.astype(jnp.bfloat16).astype(jnp.float32)
        rest = rest - piece
        pieces = jnp.where(row == n, piece, pieces)
    buf[...] = pieces.astype(jnp.bfloat16)
    copy = pltpu.make_async_copy(buf, out_hbm.at[pl.ds(at, buf.shape[0])], sem)
    copy.start()
    copy.wait()


def attach(me, powers, divisor, chunk):
    return pl.pallas_call(
        functools.partial(attach_kernel, chunk.shape[0] - SUBLANES, divisor, len(powers)),
        out_shape=jax.ShapeDtypeStruct(chunk.shape, chunk.dtype),
        in_specs=[SMEM] * (1 + len(powers)) + [HBM],
        out_specs=HBM,
        input_output_aliases={1 + len(powers): 0},
        scratch_shapes=[pltpu.VMEM((SUBLANES, LANES), jnp.bfloat16), pltpu.SemaphoreType.DMA],
        compiler_params=PARAMS,
        name="attach",
    )(me, *powers, chunk)


def receive_kernel(chunks, blocks, sources, has_outs, is_final, *refs):
    refs = list(refs)
    arrived = [[refs.pop(0) for _ in range(count)] for count in sources]
    if max(sources) > 1:
        which_ref = refs.pop(0)
    if has_outs:
        del refs[:2]
    if is_final:
        del refs[:1]
    served_hbm, checks_hbm = refs.pop(0), refs.pop(0)
    if is_final:
        energy_ref = refs.pop(0)
        del refs[:1]
    *packed, buf, sums_buf, in_sem, out_sem, sums_sem = refs
    width = buf.shape[1]
    first, last = chunks[0][0], chunks[-1][1]
    loads = []
    if is_final:
        packed = arrived[0]
    else:
        for n, one in enumerate(arrived):
            copies = [pltpu.make_async_copy(source, packed[n], in_sem.at[n]) for source in one]
            if len(copies) > 1:
                for k, copy in enumerate(copies):
                    pl.when(which_ref[0] == k)(copy.start)
            else:
                copies[0].start()
            loads.append(copies[0])
    member = membership(blocks, width)
    for load in loads:
        load.wait()
    stores = []
    if is_final:
        pieces = packed[0][pl.ds(packed[0].shape[0] - SUBLANES, SUBLANES), :].astype(jnp.float32)
        row = lax.broadcasted_iota(jnp.int32, pieces.shape, 0)
        pieces = jnp.sum(jnp.where(row < 3, pieces, 0.0), axis=0, keepdims=True)
        energy_ref[0] = pieces[0, 0]
    for n, chunk in enumerate(chunks):
        at = 0
        for a, b in tiles(*chunk):
            rows = b - a
            here = pl.ds(a - first, rows)
            if chunk[0] == 0:
                size = -(-blocks // SUBLANES) * SUBLANES
                scale = packed[1][pl.ds(packed[1].shape[0] - size, blocks), :rows]
                raw = packed[0][...].astype(jnp.float32)
                buf[here] = (raw * spread(scale, member)).astype(jnp.bfloat16)
            else:
                unpack(packed[n], at, buf, a - first, rows)
                at += packing(rows, width)[3]
            store = pltpu.make_async_copy(buf.at[here], served_hbm.at[pl.ds(a, rows)], out_sem.at[len(stores)])
            store.start()
            stores.append(store)
            sums_buf[:, 0, a - first : b - first] = sum_blocks(member, buf[here])
    store = pltpu.make_async_copy(sums_buf, checks_hbm.at[:, :, pl.ds(first, last - first)], sums_sem)
    store.start()
    stores.append(store)
    for store in stores:
        store.wait()


def receive(arrived, which, outs, attended, shape, blocks, chunks):
    rows, width = shape
    first, last = chunks[0][0], chunks[-1][1]
    count = sum(len(tiles(*chunk)) for chunk in chunks)
    is_final = attended is not None
    sources = [len(one) for one in arrived]
    operands = [(source, VMEM if is_final else HBM) for one in arrived for source in one]
    if max(sources) > 1:
        operands.append((which, SMEM))
    aliases = {len(operands) + n: n for n in range(len(outs))}
    operands += [(out, HBM) for out in outs]
    results = [
        (jax.ShapeDtypeStruct((rows, width), jnp.bfloat16), HBM),
        (jax.ShapeDtypeStruct((blocks, 1, rows), jnp.float32), HBM),
    ]
    if is_final:
        aliases[len(operands)] = 3
        operands.append((attended, HBM))
        results.append((jax.ShapeDtypeStruct((1,), jnp.float32), SMEM))
        results.append((jax.ShapeDtypeStruct(attended.shape, attended.dtype), HBM))
    return pl.pallas_call(
        functools.partial(receive_kernel, chunks, blocks, sources, bool(outs), is_final),
        out_shape=tuple(result for result, _ in results),
        in_specs=[spec for _, spec in operands],
        out_specs=tuple(spec for _, spec in results),
        input_output_aliases=aliases,
        scratch_shapes=([] if is_final else [pltpu.VMEM(one[0].shape, jnp.bfloat16) for one in arrived])
        + [
            pltpu.VMEM((last - first, width), jnp.bfloat16),
            pltpu.VMEM((blocks, 1, last - first), jnp.float32),
            pltpu.SemaphoreType.DMA((len(chunks),)),
            pltpu.SemaphoreType.DMA((count,)),
            pltpu.SemaphoreType.DMA,
        ],
        compiler_params=PARAMS,
    )(*[operand for operand, _ in operands])


def attend_kernel(lengths_ref, queries_ref, keys_hbm, values_hbm, out_hbm, keys_buf, values_buf, out_buf, sem, out_sem):
    seqs, slots_len, width = keys_hbm.shape
    span = queries_ref.shape[1]
    kv_heads = width // HEAD_SIZE
    heads = span // HEAD_SIZE
    each = span // kv_heads
    copies = []
    for seq in range(seqs):
        key_copy = pltpu.make_async_copy(keys_hbm.at[seq], keys_buf.at[seq], sem.at[0, seq])
        value_copy = pltpu.make_async_copy(values_hbm.at[seq], values_buf.at[seq], sem.at[1, seq])
        key_copy.start()
        value_copy.start()
        copies.append((key_copy, value_copy))
    at = lax.broadcasted_iota(jnp.int32, (heads, span), 1) - HEAD_SIZE * lax.broadcasted_iota(
        jnp.int32, (heads, span), 0
    )
    own = (at >= 0) & (at < HEAD_SIZE)
    column = lax.broadcasted_iota(jnp.int32, (span, width), 0)
    met = column % HEAD_SIZE
    for head in range(1, kv_heads):
        met = met + jnp.where(column >= head * each, HEAD_SIZE, 0)
    fold = jnp.where(met == lax.broadcasted_iota(jnp.int32, (span, width), 1), 1.0, 0.0).astype(jnp.bfloat16)
    slot = lax.broadcasted_iota(jnp.int32, (heads, slots_len), 1)
    for seq in range(seqs):
        query = jnp.where(own, queries_ref[seq : seq + 1, :].astype(jnp.float32), 0.0).astype(jnp.bfloat16)
        query = jnp.dot(query, fold, preferred_element_type=jnp.float32).astype(jnp.bfloat16)
        copies[seq][0].wait()
        scores = lax.dot_general(
            query, keys_buf[seq], (((1,), (1,)), ((), ())), preferred_element_type=jnp.float32
        ) * HEAD_SIZE ** (-0.5)
        scores = jnp.where(slot < lengths_ref[seq], scores, jnp.float32(-1e30))
        expd = jnp.exp(scores - jnp.max(scores, axis=1, keepdims=True))
        probs = (expd / jnp.sum(expd, axis=1, keepdims=True)).astype(jnp.bfloat16)
        copies[seq][1].wait()
        mixed = jnp.dot(probs, values_buf[seq], preferred_element_type=jnp.float32).astype(jnp.bfloat16)
        mixed = lax.dot_general(mixed, fold, (((1,), (1,)), ((), ())), preferred_element_type=jnp.float32)
        mixed = jnp.sum(jnp.where(own, mixed, 0.0), axis=0, keepdims=True)
        out_buf[seq : seq + 1, :] = mixed.astype(jnp.bfloat16)
    copy = pltpu.make_async_copy(out_buf, out_hbm, out_sem)
    copy.start()
    copy.wait()


def attend(queries, keys, values, lengths):
    return pl.pallas_call(
        attend_kernel,
        out_shape=jax.ShapeDtypeStruct(queries.shape, jnp.bfloat16),
        in_specs=[SMEM, VMEM, HBM, HBM],
        out_specs=HBM,
        scratch_shapes=[
            pltpu.VMEM(keys.shape, jnp.bfloat16),
            pltpu.VMEM(values.shape, jnp.bfloat16),
            pltpu.VMEM(queries.shape, jnp.bfloat16),
            pltpu.SemaphoreType.DMA((2, keys.shape[0])),
            pltpu.SemaphoreType.DMA,
        ],
        compiler_params=PARAMS,
        name="attend",
    )(lengths, queries, keys, values)


def shift(value, pairs, axis="blk"):
    return lax.ppermute(value, axis, pairs)


def plan(rows, relayed):
    if relayed:
        half = (rows // 2 + FIRST) // SUBLANES * SUBLANES
        marks = (0, FIRST, 2 * LANES, 3 * LANES, half, 5 * LANES, rows)
        groups = ((0, 1), (2,), (3, 4), (5,))
    else:
        marks = (0, FIRST, 3 * LANES, 5 * LANES, rows)
        groups = ((0, 1), (2,), (3,))
    return list(zip(marks[:-1], marks[1:])), (1, 2, 3) if relayed else (), groups


def refresh(distance, mant, expo, queries, keys, values, lengths):
    return refresh_from(distance, mant, expo, queries, keys, values, lengths)


def refresh_from(distance, mant, expo, queries, keys, values, lengths):
    count = lax.axis_size("blk")
    rows, width = mant.shape
    blocks = expo.shape[0]
    straight = [(i, (i + distance) % count) for i in range(count)]
    relayed = distance == 3 and count % 4 == 0
    bounds, by_relay, groups = plan(rows, relayed)
    to_relay = [(i, (i + 5) % count) for i in range(count) if i % 4 == 2]
    from_relay = [((i + 5) % count, (i + 3) % count) for i in range(count) if i % 4 == 2]
    others = [pair for pair in straight if pair[0] % 4 != 2]
    which = (lax.axis_index("blk") % 4 == 1).astype(jnp.int32).reshape(1)

    me = lax.axis_index("tp").reshape(1)

    sizes = [packed_rows(a, b, width) for a, b in bounds]
    sizes[1] += -(-blocks // SUBLANES) * SUBLANES
    sizes[-1] += SUBLANES
    power = jnp.zeros((1,), jnp.float32)
    fresh = [mant[: bounds[0][1]]]
    some, power = dequantize(mant, expo, power, bounds[1:2], sizes[1:2], scaled=bounds[0])
    fresh += some
    some, power = dequantize(mant, expo, power, bounds[2:], sizes[2:], counted=bounds[:1])
    fresh += some
    shards = lax.axis_size("tp")
    powers = [power] + [shift(power, [(i, (i + n) % shards) for i in range(shards)], "tp") for n in range(1, shards)]
    fresh[-1] = attach(me, powers, float(rows * shards * width), fresh[-1])
    arrived = []
    for n, chunk in enumerate(fresh):
        if n in by_relay:
            onward = shift(shift(chunk, to_relay), from_relay)
            arrived.append((shift(chunk, others), onward))
        else:
            arrived.append((shift(chunk, straight),))
    attended = attend(queries, keys, values, lengths)
    outs = []
    for group in groups:
        final = group[-1] == len(bounds) - 1
        outs = receive(
            [arrived[n] for n in group],
            which,
            outs,
            attended if final else None,
            (rows, width),
            blocks,
            [bounds[n] for n in group],
        )
    served, checks, energy, attended = outs
    return served, jnp.transpose(checks, (1, 2, 0)), energy, attended


def local(mantissa, exponent, home, queries, keys, values, lengths):
    rows, width = mantissa.shape[1:]
    mant = mantissa.reshape(rows, width)
    expo = jnp.transpose(exponent, (2, 0, 1))
    branches = [functools.partial(refresh, r) for r in range(1, LARGEST_DISTANCE + 1)]
    served, checks, energy, attended = lax.switch(
        home[0] - 1, branches, mant, expo, queries, keys, values, lengths
    )
    return served[None], checks, energy, attended


def solution(mesh):
    placed = (
        P("blk", "tp", None),
        P("blk", "tp", None),
        P(),
        P("blk", "tp"),
        P("blk", None, "tp"),
        P("blk", None, "tp"),
        P("blk"),
    )
    return jax.shard_map(
        local,
        mesh=mesh,
        in_specs=placed,
        out_specs=(P("blk", "tp", None), P("blk", "tp", None), P("blk"), P("blk", "tp")),
        check_vma=False,
    )
```

time: 218 us -> 99.3 us (0.46)
  waiting for transfers between devices: 142 us -> 37.8 us
  local copies, waits for them, and re-layouts: 36.7 us -> 0.93 us
  Pallas kernels: 0 us -> 30 us
  starting transfers between devices: 2.97 us -> 27.9 us
  other arithmetic: 16.3 us -> 0 us
  blocking collectives: 12.8 us -> 0 us
  between operations: 5.06 us -> 1.48 us
    ppermute x2 -> x15, waiting for transfers between devices: 142 us -> 37.8 us  [shift(): return lax.ppermute(value, axis, pairs)]
    pallas_call x0 -> x8, Pallas kernels: none -> 30 us  [the longest x2 12.2 us: dequantize(): pl.pallas_call(functools.partial(dequantize_kernel, chunks, scaled, count...]
    ppermute x2 -> x15, starting transfers between devices: 2.97 us -> 27.9 us  [shift(): return lax.ppermute(value, axis, pairs)]
    while x4 -> x0, local copies, waits for them, and re-layouts: 22 us -> none
    psum x1 -> x0, blocking collectives: 12.8 us -> none  [local(): energy = lax.psum(jnp.sum(wide * wide), 'tp') / (F * D)]
    unnamed x4 -> x0, local copies, waits for them, and re-layouts: 12.4 us -> none
    reduce_sum x2 -> x0, other arithmetic: 8.9 us -> none  [the longest x1 5.13 us: local(): energy = lax.psum(jnp.sum(wide * wide), 'tp') / (F * D)]
    convert_element_type x1 -> x0, other arithmetic: 5.1 us -> none  [local(): fresh = fresh.reshape(rows, width).astype(jnp.bfloat16)]
  transfers between devices with their start and end apart: 2 -> 15, of which waited for: 2 -> 5; matrix products, arithmetic and copies ran while one was open for 0% -> 0% of each run, Pallas kernels for 0% -> 23%
where the time goes in v1:
time: 99.3 us; the launch traced here: 98.9 us
  waiting for transfers between devices  37.8 us (38%)
  Pallas kernels  30 us (30%)
  starting transfers between devices  27.9 us (28%)
  between operations  1.48 us (1%)
    ppermute x15, waiting for transfers between devices, shift(): return lax.ppermute(value, axis, pairs)  37.8 us
    ppermute x15, starting transfers between devices, shift(): return lax.ppermute(value, axis, pairs)  27.9 us
    pallas_call x2, Pallas kernels, dequantize(): pl.pallas_call(functools.partial(dequantize_kernel, chunks, scaled, count...  12.2 us
    pallas_call x4, Pallas kernels, receive(): pl.pallas_call(functools.partial(receive_kernel, chunks, blocks, sources,...  9.12 us
    pallas_call x1, Pallas kernels, attend(): pl.pallas_call(attend_kernel, out_shape=jax.ShapeDtypeStruct(queries.shap...  5.51 us
    pallas_call x1, Pallas kernels, attach(): pl.pallas_call(functools.partial(attach_kernel, chunk.shape[0] - SUBLANES...  3.12 us
  transfers between devices with their start and end apart: 15, of which 5 were waited for; matrix products, arithmetic and copies ran while one was open for 0% of the time, Pallas kernels for 23%

profile of v1, /device:TPU:0, one launch (start us, length us, event | category | flops | bytes accessed | tf_op | source)
XLA Modules:
  0.0 98.9 jit_solution(5050183663346189650)
XLA Ops:
  1.3 97.4 %conditional.1 = (bf16[720,2880]{1,0:T(8,128)(2,1)}, f32[1,720,90]{1,0,2:T(1,128)}, f32[1]{0:T(128)}, bf16[4,1024]{1,0:T(4,128)(2,1)}) conditional(s32[]{:T(128)} %bitcast.7, (bf16[720,2880]{1,0:T(8,128)(2,1)}, s32[90,1,720]{2,1,0:T(1,128)}, s32[4]{0:T(128)}, bf16[4,1024]{1,0:T(4,128)(2,1)}, bf16[4,2048,128]{2,1,0:T(8,128)(2,1)}, ...), branch_computations={%region_0.0_spmd, %region_1.0_spmd, %region_2.3_spmd} | conditional | flops 18 | bytes 59147860 | solution.py:423
  1.5 0.0 copy-start.5
  1.5 0.0 copy-start.8
  1.6 4.6 %branch_2_fun.6 = (bf16[3344,128]{1,0:T(8,128)(2,1)}, f32[1]{0:T(128)}) custom-call(bf16[720,2880]{1,0:T(8,128)(2,1)} %get-tuple-element.74.mant_hbm, s32[90,1,720]{2,1,0:T(1,128)} %get-tuple-element.75.expo_ref, f32[1]{0:T(128)} %constant.38.clone.before_ref), custom_call_target="tpu_custom_call" | custom-call | tf_op jit(solution)/shard_map/cond/branch_2_fun/pallas_call | solution.py:136
  6.2 0.0 copy-start.11
  6.2 0.0 copy-start.14
  6.2 1.6 %collective-permute-start.27 = (bf16[3344,128]{1,0:T(8,128)(2,1)}, bf16[3344,128]{1,0:T(8,128)(2,1)}, u32[]{:S(2)}, u32[]{:S(2)}) collective-permute-start(bf16[3344,128]{1,0:T(8,128)(2,1)} %get-tuple-element.82), channel_id=1, source_target_pairs={{8,28},{24,12},{9,29},{25,13},{10,30},{26,14},{11,31},{27,15}} | collective-permute-start | bytes 2568200 | tf_op jit(solution)/shard_map/cond/branch_2_fun/ppermute | solution.py:350
  7.8 0.0 copy-done.5
  7.8 0.0 copy-done.8
  7.8 7.6 %branch_2_fun.7 = (bf16[2880,128]{1,0:T(8,128)(2,1)}, bf16[1808,128]{1,0:T(8,128)(2,1)S(1)}, bf16[3968,128]{1,0:T(8,128)(2,1)}, bf16[1824,128]{1,0:T(8,128)(2,1)}, f32[1]{0:T(128)}) custom-call(bf16[720,2880]{1,0:T(8,128)(2,1)S(1)} %copy-done.5, s32[90,1,720]{2,1,0:T(1,128)S(1)} %copy-done.8, f32[1]{0:T(128)} %get-tuple-element.76.before_ref), custom_call_target="tpu_custom_call" | custom-call | tf_op jit(solution)/shard_map/cond/branch_2_fun/pallas_call | solution.py:136
  15.5 0.0 copy-start.2
  15.5 1.5 %collective-permute-start.19 = (bf16[1808,128]{1,0:T(8,128)(2,1)S(1)}, bf16[1808,128]{1,0:T(8,128)(2,1)}, u32[]{:S(2)}, u32[]{:S(2)}) collective-permute-start(bf16[1808,128]{1,0:T(8,128)(2,1)S(1)} %get-tuple-element.79), channel_id=1, source_target_pairs={{8,28},{24,12},{9,29},{25,13},{10,30},{26,14},{11,31},{27,15}} | collective-permute-start | bytes 1388552 | tf_op jit(solution)/shard_map/cond/branch_2_fun/ppermute | solution.py:350
  17.0 2.0 %collective-permute-start.25 = (bf16[112,2880]{1,0:T(8,128)(2,1)S(1)}, bf16[112,2880]{1,0:T(8,128)(2,1)S(1)}, u32[]{:S(2)}, u32[]{:S(2)}) collective-permute-start(bf16[112,2880]{1,0:T(8,128)(2,1)S(1)} %slice.10), channel_id=1, source_target_pairs={{0,12},{4,16},{8,20},{12,24},{16,28},{20,0},{24,4},{28,8},{1,13},{... | collective-permute-start | bytes 1935368 | tf_op jit(solution)/shard_map/cond/branch_2_fun/ppermute | solution.py:350
  19.0 1.5 %collective-permute-start.23 = (bf16[2880,128]{1,0:T(8,128)(2,1)}, bf16[2880,128]{1,0:T(8,128)(2,1)}, u32[]{:S(2)}, u32[]{:S(2)}) collective-permute-start(bf16[2880,128]{1,0:T(8,128)(2,1)} %get-tuple-element.81), channel_id=1, source_target_pairs={{8,28},{24,12},{9,29},{25,13},{10,30},{26,14},{11,31},{27,15}} | collective-permute-start | bytes 2211848 | tf_op jit(solution)/shard_map/cond/branch_2_fun/ppermute | solution.py:350
  20.5 1.6 %collective-permute-start.14 = (f32[1]{0:T(128)}, f32[1]{0:T(128)}, u32[]{:S(2)}, u32[]{:S(2)}) collective-permute-start(f32[1]{0:T(128)} %get-tuple-element.77.refs_0_), channel_id=1, source_target_pairs={{0,1},{1,2},{2,3},{3,0},{4,5},{5,6},{6,7},{7,4},{8,9},{9,10},{10,1... | collective-permute-start | bytes 20 | tf_op jit(solution)/shard_map/cond/branch_2_fun/ppermute | solution.py:350
  22.1 3.9 %collective-permute-done.14.refs_1_ = f32[1]{0:T(128)} collective-permute-done((f32[1]{0:T(128)}, f32[1]{0:T(128)}, u32[]{:S(2)}, u32[]{:S(2)}) %collective-permute-start.14) | collective-permute-done | bytes 36 | tf_op jit(solution)/shard_map/cond/branch_2_fun/ppermute | solution.py:350
  26.0 0.8 collective-permute-start.15
  26.8 3.9 %collective-permute-done.15.refs_2_ = f32[1]{0:T(128)} collective-permute-done((f32[1]{0:T(128)}, f32[1]{0:T(128)}, u32[]{:S(2)}, u32[]{:S(2)}) %collective-permute-start.15) | collective-permute-done | bytes 36 | tf_op jit(solution)/shard_map/cond/branch_2_fun/ppermute | solution.py:350
  30.7 1.8 %collective-permute-start.16 = (f32[1]{0:T(128)}, f32[1]{0:T(128)}, u32[]{:S(2)}, u32[]{:S(2)}) collective-permute-start(f32[1]{0:T(128)} %get-tuple-element.77.refs_0_), channel_id=1, source_target_pairs={{0,3},{1,0},{2,1},{3,2},{4,7},{5,4},{6,5},{7,6},{8,11},{9,8},{10,9... | collective-permute-start | bytes 20 | tf_op jit(solution)/shard_map/cond/branch_2_fun/ppermute | solution.py:350
  32.5 1.8 %collective-permute-done.16.refs_3_ = f32[1]{0:T(128)} collective-permute-done((f32[1]{0:T(128)}, f32[1]{0:T(128)}, u32[]{:S(2)}, u32[]{:S(2)}) %collective-permute-start.16) | collective-permute-done | bytes 36 | tf_op jit(solution)/shard_map/cond/branch_2_fun/ppermute | solution.py:350
  34.3 2.7 %collective-permute-start.26 = (bf16[3344,128]{1,0:T(8,128)(2,1)}, bf16[3344,128]{1,0:T(8,128)(2,1)S(1)}, u32[]{:S(2)}, u32[]{:S(2)}) collective-permute-start(bf16[3344,128]{1,0:T(8,128)(2,1)} %get-tuple-element.82), channel_id=1, source_target_pairs={{0,12},{4,16},{12,24},{16,28},{20,0},{28,8},{1,13},{5,17},{13,25},... | collective-permute-start | bytes 2568200 | tf_op jit(solution)/shard_map/cond/branch_2_fun/ppermute | solution.py:350
  37.1 0.0 collective-permute-done.27
  37.1 0.7 collective-permute-start.28
  37.8 0.0 collective-permute-done.19
  37.8 8.7 %collective-permute-start.22 = (bf16[2880,128]{1,0:T(8,128)(2,1)}, bf16[2880,128]{1,0:T(8,128)(2,1)S(1)}, u32[]{:S(2)}, u32[]{:S(2)}) collective-permute-start(bf16[2880,128]{1,0:T(8,128)(2,1)} %get-tuple-element.81), channel_id=1, source_target_pairs={{0,12},{4,16},{12,24},{16,28},{20,0},{28,8},{1,13},{5,17},{13,25},... | collective-permute-start | bytes 2211848 | tf_op jit(solution)/shard_map/cond/branch_2_fun/ppermute | solution.py:350
  46.6 0.0 collective-permute-done.25.refs_0_
  46.6 0.0 copy-done.2
  46.6 0.0 copy-start
  46.6 0.8 copy-done
  47.4 0.0 collective-permute-start.21
  47.5 0.0 collective-permute-done.23
  47.5 1.5 %collective-permute-start.24 = (bf16[2880,128]{1,0:T(8,128)(2,1)}, bf16[2880,128]{1,0:T(8,128)(2,1)}, u32[]{:S(2)}, u32[]{:S(2)}) collective-permute-start(bf16[2880,128]{1,0:T(8,128)(2,1)} %collective-permute-done.23), channel_id=1, source_target_pairs={{28,20},{12,4},{29,21},{13,5},{30,22},{14,6},{31,23},{15,7}} | collective-permute-start | bytes 2211848 | tf_op jit(solution)/shard_map/cond/branch_2_fun/ppermute | solution.py:350
  49.0 3.1 %attach.5 = bf16[1824,128]{1,0:T(8,128)(2,1)} custom-call(s32[1]{0:T(128)} %bitcast.4.me_ref, f32[1]{0:T(128)} %get-tuple-element.77.refs_0_, f32[1]{0:T(128)} %collective-permute-done.14.refs_1_, f32[1]{0:T(128)} %collective-permute-done.15.refs_2_, f32[1]{0:T(128)} %collective-permute-done.16.refs_3_, ...), custom_call_target="tpu_custom_call", output_to_operand_aliasing={{}: (5, {})} | custom-call | tf_op jit(solution)/shard_map/cond/branch_2_fun/attach/pallas_call | solution.py:177
  52.1 13.8 %collective-permute-done.22.refs_0_ = bf16[2880,128]{1,0:T(8,128)(2,1)S(1)} collective-permute-done((bf16[2880,128]{1,0:T(8,128)(2,1)}, bf16[2880,128]{1,0:T(8,128)(2,1)S(1)}, u32[]{:S(2)}, u32[]{:S(2)}) %collective-permute-start.22) | collective-permute-done | bytes 737312 | tf_op jit(solution)/shard_map/cond/branch_2_fun/ppermute | solution.py:350
  65.9 0.0 collective-permute-start.17
  65.9 0.0 collective-permute-done.26.refs_1_
  65.9 1.9 %collective-permute-start.18 = (bf16[1808,128]{1,0:T(8,128)(2,1)}, bf16[1808,128]{1,0:T(8,128)(2,1)}, u32[]{:S(2)}, u32[]{:S(2)}) collective-permute-start(bf16[1808,128]{1,0:T(8,128)(2,1)} %copy-done.2), channel_id=1, source_target_pairs={{0,12},{4,16},{12,24},{16,28},{20,0},{28,8},{1,13},{5,17},{13,25},... | collective-permute-start | bytes 1388552 | tf_op jit(solution)/shard_map/cond/branch_2_fun/ppermute | solution.py:350
  67.8 0.0 collective-permute-done.28.refs_2_
  67.8 1.4 %collective-permute-start.20 = (bf16[1808,128]{1,0:T(8,128)(2,1)}, bf16[1808,128]{1,0:T(8,128)(2,1)}, u32[]{:S(2)}, u32[]{:S(2)}) collective-permute-start(bf16[1808,128]{1,0:T(8,128)(2,1)} %collective-permute-done.19), channel_id=1, source_target_pairs={{28,20},{12,4},{29,21},{13,5},{30,22},{14,6},{31,23},{15,7}} | collective-permute-start | bytes 1388552 | tf_op jit(solution)/shard_map/cond/branch_2_fun/ppermute | solution.py:350
  69.3 0.0 copy-start.1
  69.3 0.0 copy-done.11
  69.3 0.0 copy-done.14
  69.3 5.5 %attend.5.refs_3_ = bf16[4,1024]{1,0:T(4,128)(2,1)} custom-call(s32[4]{0:T(128)S(1)} %copy-done.14, bf16[4,1024]{1,0:T(4,128)(2,1)S(1)} %copy-done.11, bf16[4,2048,128]{2,1,0:T(8,128)(2,1)} %get-tuple-element.91.keys_hbm, bf16[4,2048,128]{2,1,0:T(8,128)(2,1)} %get-tuple-element.92.values_hbm), custom_call_target="tpu_custom_call" | custom-call | tf_op jit(solution)/shard_map/cond/branch_2_fun/attend/pallas_call | solution.py:332
  74.8 0.0 copy-done.1
  74.8 2.4 %branch_2_fun.8 = (bf16[720,2880]{1,0:T(8,128)(2,1)}, f32[90,1,720]{2,1,0:T(1,128)}) custom-call(bf16[112,2880]{1,0:T(8,128)(2,1)S(1)} %copy-done.1, bf16[3344,128]{1,0:T(8,128)(2,1)S(1)} %collective-permute-done.26.refs_1_, bf16[3344,128]{1,0:T(8,128)(2,1)S(1)} %collective-permute-done.28.refs_2_, s32[1]{0:T(128)} %bitcast.5.refs_3_.refs_2_), custom_call_target="tpu_custom_call" | custom-call | tf_op jit(solution)/shard_map/cond/branch_2_fun/pallas_call | solution.py:270
  77.2 0.0 collective-permute-done.24.refs_1_
  77.2 1.6 %branch_2_fun.9 = (bf16[720,2880]{1,0:T(8,128)(2,1)}, f32[90,1,720]{2,1,0:T(1,128)}) custom-call(bf16[2880,128]{1,0:T(8,128)(2,1)S(1)} %collective-permute-done.22.refs_0_, bf16[2880,128]{1,0:T(8,128)(2,1)} %collective-permute-done.24.refs_1_, s32[1]{0:T(128)} %bitcast.5.refs_3_.refs_2_, ...), custom_call_target="tpu_custom_call", output_to_operand_aliasing={{0}: (3, {}), {1}: (4, {})} | custom-call | tf_op jit(solution)/shard_map/cond/branch_2_fun/pallas_call | solution.py:270
  78.9 14.4 %collective-permute-done.18.refs_0_ = bf16[1808,128]{1,0:T(8,128)(2,1)} collective-permute-done((bf16[1808,128]{1,0:T(8,128)(2,1)}, bf16[1808,128]{1,0:T(8,128)(2,1)}, u32[]{:S(2)}, u32[]{:S(2)}) %collective-permute-start.18) | collective-permute-done | bytes 462880 | tf_op jit(solution)/shard_map/cond/branch_2_fun/ppermute | solution.py:350
  93.3 0.0 collective-permute-done.20.refs_1_
  93.3 0.0 collective-permute-done.21.refs_2_
  93.3 2.5 %branch_2_fun.10 = (bf16[720,2880]{1,0:T(8,128)(2,1)}, f32[90,1,720]{2,1,0:T(1,128)}) custom-call(bf16[1808,128]{1,0:T(8,128)(2,1)} %collective-permute-done.18.refs_0_, bf16[1808,128]{1,0:T(8,128)(2,1)} %collective-permute-done.20.refs_1_, bf16[3968,128]{1,0:T(8,128)(2,1)S(1)} %collective-permute-done.21.refs_2_, ...), custom_call_target="tpu_custom_call", output_to_operand_aliasing={{0}: (4, {}), {1}: (5, {})} | custom-call | tf_op jit(solution)/shard_map/cond/branch_2_fun/pallas_call | solution.py:270
  95.9 0.0 collective-permute-done.17.refs_0_
  95.9 2.5 %branch_2_fun.11 = (bf16[720,2880]{1,0:T(8,128)(2,1)}, f32[90,1,720]{2,1,0:T(1,128)}, f32[1]{0:T(128)}, bf16[4,1024]{1,0:T(4,128)(2,1)}) custom-call(bf16[1824,128]{1,0:T(8,128)(2,1)} %collective-permute-done.17.refs_0_, bf16[720,2880]{1,0:T(8,128)(2,1)} %get-tuple-element.87.refs_1_, ...), custom_call_target="tpu_custom_call", output_to_operand_aliasing={{0}: (1, {}), {1}: (2, {}), {3}: (3, {})} | custom-call | tf_op jit(solution)/shard_map/cond/branch_2_fun/pallas_call | solution.py:270
  (1 shorter events, 0.0 us)
Async XLA Ops:
  1.5 6.3 %copy-start.5 = (bf16[720,2880]{1,0:T(8,128)(2,1)S(1)}, bf16[720,2880]{1,0:T(8,128)(2,1)}, u32[]{:S(2)}) copy-start(bf16[720,2880]{1,0:T(8,128)(2,1)} %get-tuple-element.74.mant_hbm) | copy-start | bytes 12441604 | tf_op jit(solution)/shard_map/cond
  1.5 6.3 %copy-start.8 = (s32[90,1,720]{2,1,0:T(1,128)S(1)}, s32[90,1,720]{2,1,0:T(1,128)}, u32[]{:S(2)}) copy-start(s32[90,1,720]{2,1,0:T(1,128)} %get-tuple-element.75.expo_ref) | copy-start | bytes 777604 | tf_op jit(solution)/shard_map/cond
  6.2 63.1 %copy-start.11 = (bf16[4,1024]{1,0:T(4,128)(2,1)S(1)}, bf16[4,1024]{1,0:T(4,128)(2,1)}, u32[]{:S(2)}) copy-start(bf16[4,1024]{1,0:T(4,128)(2,1)} %get-tuple-element.90.queries_ref) | copy-start | bytes 24580 | tf_op jit(solution)/shard_map/cond
  6.2 63.1 %copy-start.14 = (s32[4]{0:T(128)S(1)}, s32[4]{0:T(128)}, u32[]{:S(2)}) copy-start(s32[4]{0:T(128)} %get-tuple-element.89.lengths_ref) | copy-start | bytes 52 | tf_op jit(solution)/shard_map/cond
  6.2 30.8 %collective-permute-start.27 = (bf16[3344,128]{1,0:T(8,128)(2,1)}, bf16[3344,128]{1,0:T(8,128)(2,1)}, u32[]{:S(2)}, u32[]{:S(2)}) collective-permute-start(bf16[3344,128]{1,0:T(8,128)(2,1)} %get-tuple-element.82), channel_id=1, source_target_pairs={{8,28},{24,12},{9,29},{25,13},{10,30},{26,14},{11,31},{27,15}} | collective-permute-start | bytes 2568200 | tf_op jit(solution)/shard_map/cond/branch_2_fun/ppermute | solution.py:350
  15.5 31.1 %copy-start.2 = (bf16[1808,128]{1,0:T(8,128)(2,1)}, bf16[1808,128]{1,0:T(8,128)(2,1)S(1)}, u32[]{:S(2)}) copy-start(bf16[1808,128]{1,0:T(8,128)(2,1)S(1)} %get-tuple-element.79) | copy-start | bytes 1388548 | tf_op jit(solution)/shard_map/cond
  15.5 22.3 %collective-permute-start.19 = (bf16[1808,128]{1,0:T(8,128)(2,1)S(1)}, bf16[1808,128]{1,0:T(8,128)(2,1)}, u32[]{:S(2)}, u32[]{:S(2)}) collective-permute-start(bf16[1808,128]{1,0:T(8,128)(2,1)S(1)} %get-tuple-element.79), channel_id=1, source_target_pairs={{8,28},{24,12},{9,29},{25,13},{10,30},{26,14},{11,31},{27,15}} | collective-permute-start | bytes 1388552 | tf_op jit(solution)/shard_map/cond/branch_2_fun/ppermute | solution.py:350
  17.0 29.6 %collective-permute-start.25 = (bf16[112,2880]{1,0:T(8,128)(2,1)S(1)}, bf16[112,2880]{1,0:T(8,128)(2,1)S(1)}, u32[]{:S(2)}, u32[]{:S(2)}) collective-permute-start(bf16[112,2880]{1,0:T(8,128)(2,1)S(1)} %slice.10), channel_id=1, source_target_pairs={{0,12},{4,16},{8,20},{12,24},{16,28},{20,0},{24,4},{28,8},{1,13},{... | collective-permute-start | bytes 1935368 | tf_op jit(solution)/shard_map/cond/branch_2_fun/ppermute | solution.py:350
  19.0 28.5 %collective-permute-start.23 = (bf16[2880,128]{1,0:T(8,128)(2,1)}, bf16[2880,128]{1,0:T(8,128)(2,1)}, u32[]{:S(2)}, u32[]{:S(2)}) collective-permute-start(bf16[2880,128]{1,0:T(8,128)(2,1)} %get-tuple-element.81), channel_id=1, source_target_pairs={{8,28},{24,12},{9,29},{25,13},{10,30},{26,14},{11,31},{27,15}} | collective-permute-start | bytes 2211848 | tf_op jit(solution)/shard_map/cond/branch_2_fun/ppermute | solution.py:350
  20.5 5.5 %collective-permute-start.14 = (f32[1]{0:T(128)}, f32[1]{0:T(128)}, u32[]{:S(2)}, u32[]{:S(2)}) collective-permute-start(f32[1]{0:T(128)} %get-tuple-element.77.refs_0_), channel_id=1, source_target_pairs={{0,1},{1,2},{2,3},{3,0},{4,5},{5,6},{6,7},{7,4},{8,9},{9,10},{10,1... | collective-permute-start | bytes 20 | tf_op jit(solution)/shard_map/cond/branch_2_fun/ppermute | solution.py:350
  26.0 4.7 %collective-permute-start.15 = (f32[1]{0:T(128)}, f32[1]{0:T(128)}, u32[]{:S(2)}, u32[]{:S(2)}) collective-permute-start(f32[1]{0:T(128)} %get-tuple-element.77.refs_0_), channel_id=1, source_target_pairs={{0,2},{1,3},{2,0},{3,1},{4,6},{5,7},{6,4},{7,5},{8,10},{9,11},{10,... | collective-permute-start | bytes 20 | tf_op jit(solution)/shard_map/cond/branch_2_fun/ppermute | solution.py:350
  30.7 3.7 %collective-permute-start.16 = (f32[1]{0:T(128)}, f32[1]{0:T(128)}, u32[]{:S(2)}, u32[]{:S(2)}) collective-permute-start(f32[1]{0:T(128)} %get-tuple-element.77.refs_0_), channel_id=1, source_target_pairs={{0,3},{1,0},{2,1},{3,2},{4,7},{5,4},{6,5},{7,6},{8,11},{9,8},{10,9... | collective-permute-start | bytes 20 | tf_op jit(solution)/shard_map/cond/branch_2_fun/ppermute | solution.py:350
  34.3 31.6 %collective-permute-start.26 = (bf16[3344,128]{1,0:T(8,128)(2,1)}, bf16[3344,128]{1,0:T(8,128)(2,1)S(1)}, u32[]{:S(2)}, u32[]{:S(2)}) collective-permute-start(bf16[3344,128]{1,0:T(8,128)(2,1)} %get-tuple-element.82), channel_id=1, source_target_pairs={{0,12},{4,16},{12,24},{16,28},{20,0},{28,8},{1,13},{5,17},{13,25},... | collective-permute-start | bytes 2568200 | tf_op jit(solution)/shard_map/cond/branch_2_fun/ppermute | solution.py:350
  37.1 30.7 %collective-permute-start.28 = (bf16[3344,128]{1,0:T(8,128)(2,1)}, bf16[3344,128]{1,0:T(8,128)(2,1)S(1)}, u32[]{:S(2)}, u32[]{:S(2)}) collective-permute-start(bf16[3344,128]{1,0:T(8,128)(2,1)} %collective-permute-done.27), channel_id=1, source_target_pairs={{28,20},{12,4},{29,21},{13,5},{30,22},{14,6},{31,23},{15,7}} | collective-permute-start | bytes 2568200 | tf_op jit(solution)/shard_map/cond/branch_2_fun/ppermute | solution.py:350
  37.8 28.1 %collective-permute-start.22 = (bf16[2880,128]{1,0:T(8,128)(2,1)}, bf16[2880,128]{1,0:T(8,128)(2,1)S(1)}, u32[]{:S(2)}, u32[]{:S(2)}) collective-permute-start(bf16[2880,128]{1,0:T(8,128)(2,1)} %get-tuple-element.81), channel_id=1, source_target_pairs={{0,12},{4,16},{12,24},{16,28},{20,0},{28,8},{1,13},{5,17},{13,25},... | collective-permute-start | bytes 2211848 | tf_op jit(solution)/shard_map/cond/branch_2_fun/ppermute | solution.py:350
  46.6 0.9 copy-start
  47.4 45.9 %collective-permute-start.21 = (bf16[3968,128]{1,0:T(8,128)(2,1)}, bf16[3968,128]{1,0:T(8,128)(2,1)S(1)}, u32[]{:S(2)}, u32[]{:S(2)}) collective-permute-start(bf16[3968,128]{1,0:T(8,128)(2,1)} %get-tuple-element.80), channel_id=1, source_target_pairs={{0,12},{4,16},{8,20},{12,24},{16,28},{20,0},{24,4},{28,8},{1,13},{... | collective-permute-start | bytes 3047432 | tf_op jit(solution)/shard_map/cond/branch_2_fun/ppermute | solution.py:350
  47.5 29.8 %collective-permute-start.24 = (bf16[2880,128]{1,0:T(8,128)(2,1)}, bf16[2880,128]{1,0:T(8,128)(2,1)}, u32[]{:S(2)}, u32[]{:S(2)}) collective-permute-start(bf16[2880,128]{1,0:T(8,128)(2,1)} %collective-permute-done.23), channel_id=1, source_target_pairs={{28,20},{12,4},{29,21},{13,5},{30,22},{14,6},{31,23},{15,7}} | collective-permute-start | bytes 2211848 | tf_op jit(solution)/shard_map/cond/branch_2_fun/ppermute | solution.py:350
  65.9 30.0 %collective-permute-start.17 = (bf16[1824,128]{1,0:T(8,128)(2,1)}, bf16[1824,128]{1,0:T(8,128)(2,1)}, u32[]{:S(2)}, u32[]{:S(2)}) collective-permute-start(bf16[1824,128]{1,0:T(8,128)(2,1)} %attach.5), channel_id=1, source_target_pairs={{0,12},{4,16},{8,20},{12,24},{16,28},{20,0},{24,4},{28,8},{1,13},{... | collective-permute-start | bytes 1400840 | tf_op jit(solution)/shard_map/cond/branch_2_fun/ppermute | solution.py:350
  65.9 27.4 %collective-permute-start.18 = (bf16[1808,128]{1,0:T(8,128)(2,1)}, bf16[1808,128]{1,0:T(8,128)(2,1)}, u32[]{:S(2)}, u32[]{:S(2)}) collective-permute-start(bf16[1808,128]{1,0:T(8,128)(2,1)} %copy-done.2), channel_id=1, source_target_pairs={{0,12},{4,16},{12,24},{16,28},{20,0},{28,8},{1,13},{5,17},{13,25},... | collective-permute-start | bytes 1388552 | tf_op jit(solution)/shard_map/cond/branch_2_fun/ppermute | solution.py:350
  67.8 25.5 %collective-permute-start.20 = (bf16[1808,128]{1,0:T(8,128)(2,1)}, bf16[1808,128]{1,0:T(8,128)(2,1)}, u32[]{:S(2)}, u32[]{:S(2)}) collective-permute-start(bf16[1808,128]{1,0:T(8,128)(2,1)} %collective-permute-done.19), channel_id=1, source_target_pairs={{28,20},{12,4},{29,21},{13,5},{30,22},{14,6},{31,23},{15,7}} | collective-permute-start | bytes 1388552 | tf_op jit(solution)/shard_map/cond/branch_2_fun/ppermute | solution.py:350
  69.3 5.5 %copy-start.1 = (bf16[112,2880]{1,0:T(8,128)(2,1)S(1)}, bf16[112,2880]{1,0:T(8,128)(2,1)}, u32[]{:S(2)}) copy-start(bf16[112,2880]{1,0:T(8,128)(2,1)} %copy-done) | copy-start | bytes 1935364 | tf_op jit(solution)/shard_map/cond

commit v2 on v1

--- a/solution.py
+++ b/solution.py
@@ -12,7 +12,7 @@
 LARGEST_DISTANCE = 3
 LANES = 128
 SUBLANES = 16
-FIRST = 112
+FIRST = {1: 112, 2: 64, 3: 112}
 HBM = pl.BlockSpec(memory_space=pltpu.HBM)
 VMEM = pl.BlockSpec(memory_space=pltpu.VMEM)
 SMEM = pl.BlockSpec(memory_space=pltpu.SMEM)
@@ -76,6 +76,44 @@
 
 def sum_blocks(member, served):
     return lax.dot_general(member, served, (((1,), (1,)), ((), ())), preferred_element_type=jnp.float32)
+
+
+def take_kernel(spans, source_hbm, out_hbm, raw, packed, in_sem, out_sem):
+    width = source_hbm.shape[1]
+    loads, stores = [], []
+    for n, (a, b) in enumerate(spans):
+        load = pltpu.make_async_copy(source_hbm.at[pl.ds(a, b - a)], raw.at[pl.ds(a, b - a)], in_sem.at[n])
+        load.start()
+        loads.append(load)
+    at = 0
+    for n, (a, b) in enumerate(spans):
+        size = packing(b - a, width)[3]
+        loads[n].wait()
+        pack(raw[pl.ds(a, b - a)], packed, at)
+        store = pltpu.make_async_copy(packed.at[pl.ds(at, size)], out_hbm.at[pl.ds(at, size)], out_sem.at[n])
+        store.start()
+        stores.append(store)
+        at += size
+    for store in stores:
+        store.wait()
+
+
+def take(source, last, size):
+    spans = tiles(0, last)
+    return pl.pallas_call(
+        functools.partial(take_kernel, spans),
+        out_shape=jax.ShapeDtypeStruct((size, LANES), source.dtype),
+        in_specs=[HBM],
+        out_specs=HBM,
+        scratch_shapes=[
+            pltpu.VMEM((last, source.shape[1]), source.dtype),
+            pltpu.VMEM((size, LANES), source.dtype),
+            pltpu.SemaphoreType.DMA((len(spans),)),
+            pltpu.SemaphoreType.DMA((len(spans),)),
+        ],
+        compiler_params=PARAMS,
+        name="take",
+    )(source)
 
 
 def dequantize_kernel(chunks, scaled, counted, mant_hbm, expo_ref, before_ref, *refs):
@@ -147,6 +185,7 @@
             pltpu.SemaphoreType.DMA,
         ],
         compiler_params=PARAMS,
+        name="dequantize_second" if scaled else "dequantize_rest",
     )(mant, expo, before)
     return fresh, power
 
@@ -186,7 +225,7 @@
     )(me, *powers, chunk)
 
 
-def receive_kernel(chunks, blocks, sources, has_outs, is_final, *refs):
+def receive_kernel(chunks, blocks, sources, has_outs, is_final, direct, *refs):
     refs = list(refs)
     arrived = [[refs.pop(0) for _ in range(count)] for count in sources]
     if max(sources) > 1:
@@ -203,8 +242,8 @@
     width = buf.shape[1]
     first, last = chunks[0][0], chunks[-1][1]
     loads = []
-    if is_final:
-        packed = arrived[0]
+    if direct:
+        packed = [one[0] for one in arrived]
     else:
         for n, one in enumerate(arrived):
             copies = [pltpu.make_async_copy(source, packed[n], in_sem.at[n]) for source in one]
@@ -215,27 +254,20 @@
                 copies[0].start()
             loads.append(copies[0])
     member = membership(blocks, width)
-    for load in loads:
-        load.wait()
     stores = []
-    if is_final:
-        pieces = packed[0][pl.ds(packed[0].shape[0] - SUBLANES, SUBLANES), :].astype(jnp.float32)
-        row = lax.broadcasted_iota(jnp.int32, pieces.shape, 0)
-        pieces = jnp.sum(jnp.where(row < 3, pieces, 0.0), axis=0, keepdims=True)
-        energy_ref[0] = pieces[0, 0]
     for n, chunk in enumerate(chunks):
         at = 0
+        while loads and (len(loads) == len(chunks) - n or chunk[0] == 0):
+            loads.pop(0).wait()
         for a, b in tiles(*chunk):
             rows = b - a
             here = pl.ds(a - first, rows)
+            unpack(packed[n], at, buf, a - first, rows)
+            at += packing(rows, width)[3]
             if chunk[0] == 0:
                 size = -(-blocks // SUBLANES) * SUBLANES
-                scale = packed[1][pl.ds(packed[1].shape[0] - size, blocks), :rows]
-                raw = packed[0][...].astype(jnp.float32)
-                buf[here] = (raw * spread(scale, member)).astype(jnp.bfloat16)
-            else:
-                unpack(packed[n], at, buf, a - first, rows)
-                at += packing(rows, width)[3]
+                scale = packed[1][pl.ds(packed[1].shape[0] - size, blocks), a:b]
+                buf[here] = (buf[here].astype(jnp.float32) * spread(scale, member)).astype(jnp.bfloat16)
             store = pltpu.make_async_copy(buf.at[here], served_hbm.at[pl.ds(a, rows)], out_sem.at[len(stores)])
             store.start()
             stores.append(store)
@@ -243,6 +275,11 @@
     store = pltpu.make_async_copy(sums_buf, checks_hbm.at[:, :, pl.ds(first, last - first)], sums_sem)
     store.start()
     stores.append(store)
+    if is_final:
+        pieces = packed[-1][pl.ds(packed[-1].shape[0] - SUBLANES, SUBLANES), :].astype(jnp.float32)
+        row = lax.broadcasted_iota(jnp.int32, pieces.shape, 0)
+        pieces = jnp.sum(jnp.where(row < 3, pieces, 0.0), axis=0, keepdims=True)
+        energy_ref[0] = pieces[0, 0]
     for store in stores:
         store.wait()
 
@@ -253,7 +290,8 @@
     count = sum(len(tiles(*chunk)) for chunk in chunks)
     is_final = attended is not None
     sources = [len(one) for one in arrived]
-    operands = [(source, VMEM if is_final else HBM) for one in arrived for source in one]
+    direct = is_final and max(sources) == 1
+    operands = [(source, VMEM if direct else HBM) for one in arrived for source in one]
     if max(sources) > 1:
         operands.append((which, SMEM))
     aliases = {len(operands) + n: n for n in range(len(outs))}
@@ -268,12 +306,12 @@
         results.append((jax.ShapeDtypeStruct((1,), jnp.float32), SMEM))
         results.append((jax.ShapeDtypeStruct(attended.shape, attended.dtype), HBM))
     return pl.pallas_call(
-        functools.partial(receive_kernel, chunks, blocks, sources, bool(outs), is_final),
+        functools.partial(receive_kernel, chunks, blocks, sources, bool(outs), is_final, direct),
         out_shape=tuple(result for result, _ in results),
         in_specs=[spec for _, spec in operands],
         out_specs=tuple(spec for _, spec in results),
         input_output_aliases=aliases,
-        scratch_shapes=([] if is_final else [pltpu.VMEM(one[0].shape, jnp.bfloat16) for one in arrived])
+        scratch_shapes=([] if direct else [pltpu.VMEM(one[0].shape, jnp.bfloat16) for one in arrived])
         + [
             pltpu.VMEM((last - first, width), jnp.bfloat16),
             pltpu.VMEM((blocks, 1, last - first), jnp.float32),
@@ -350,15 +388,16 @@
     return lax.ppermute(value, axis, pairs)
 
 
-def plan(rows, relayed):
+def plan(rows, distance, relayed):
+    first = FIRST[distance]
     if relayed:
-        half = (rows // 2 + FIRST) // SUBLANES * SUBLANES
-        marks = (0, FIRST, 2 * LANES, 3 * LANES, half, 5 * LANES, rows)
-        groups = ((0, 1), (2,), (3, 4), (5,))
+        half = (rows // 2 + 2 * first) // SUBLANES * SUBLANES
+        marks = (0, first, 2 * LANES, 3 * LANES, 4 * LANES, half, rows)
+        groups = ((0, 1), (2,), (3,), (4, 5))
     else:
-        marks = (0, FIRST, 3 * LANES, 5 * LANES, rows)
+        marks = (0, first, 3 * LANES, 5 * LANES, rows)
         groups = ((0, 1), (2,), (3,))
-    return list(zip(marks[:-1], marks[1:])), (1, 2, 3) if relayed else (), groups
+    return list(zip(marks[:-1], marks[1:])), (1, 2, 4) if relayed else (), groups
 
 
 def refresh(distance, mant, expo, queries, keys, values, lengths):
@@ -371,7 +410,7 @@
     blocks = expo.shape[0]
     straight = [(i, (i + distance) % count) for i in range(count)]
     relayed = distance == 3 and count % 4 == 0
-    bounds, by_relay, groups = plan(rows, relayed)
+    bounds, by_relay, groups = plan(rows, distance, relayed)
     to_relay = [(i, (i + 5) % count) for i in range(count) if i % 4 == 2]
     from_relay = [((i + 5) % count, (i + 3) % count) for i in range(count) if i % 4 == 2]
     others = [pair for pair in straight if pair[0] % 4 != 2]
@@ -383,7 +422,7 @@
     sizes[1] += -(-blocks // SUBLANES) * SUBLANES
     sizes[-1] += SUBLANES
     power = jnp.zeros((1,), jnp.float32)
-    fresh = [mant[: bounds[0][1]]]
+    fresh = [take(mant, bounds[0][1], sizes[0])]
     some, power = dequantize(mant, expo, power, bounds[1:2], sizes[1:2], scaled=bounds[0])
     fresh += some
     some, power = dequantize(mant, expo, power, bounds[2:], sizes[2:], counted=bounds[:1])

time: 99.3 us -> 95.7 us (0.964)
  waiting for transfers between devices: 37.8 us -> 28.7 us
  starting transfers between devices: 27.9 us -> 31.4 us
  Pallas kernels: 30 us -> 31.9 us
    ppermute x15, waiting for transfers between devices: 37.8 us -> 28.7 us  [shift(): return lax.ppermute(value, axis, pairs)]
    ppermute x15, starting transfers between devices: 27.9 us -> 31.4 us  [shift(): return lax.ppermute(value, axis, pairs)]
    pallas_call x0 -> x1, Pallas kernels: none -> 1.15 us  [take(): pl.pallas_call(functools.partial(take_kernel, spans), out_shape=jax.Shape...]
    pallas_call x4, Pallas kernels: 9.12 us -> 10.1 us  [receive(): pl.pallas_call(functools.partial(receive_kernel, chunks, blocks, sources,...]
  transfers between devices with their start and end apart: 15 -> 15, of which waited for: 5 -> 5; matrix products, arithmetic and copies ran while one was open for 0% -> 0% of each run, Pallas kernels for 23% -> 25%
where the time goes in v2:
time: 95.7 us; the launch traced here: 95.2 us
  Pallas kernels  31.9 us (33%)
  starting transfers between devices  31.4 us (33%)
  waiting for transfers between devices  28.7 us (30%)
  between operations  1.48 us (2%)
    ppermute x15, starting transfers between devices, shift(): return lax.ppermute(value, axis, pairs)  31.4 us
    ppermute x15, waiting for transfers between devices, shift(): return lax.ppermute(value, axis, pairs)  28.7 us
    pallas_call x2, Pallas kernels, dequantize(): pl.pallas_call(functools.partial(dequantize_kernel, chunks, scaled, count...  12.6 us
    pallas_call x4, Pallas kernels, receive(): pl.pallas_call(functools.partial(receive_kernel, chunks, blocks, sources,...  10.1 us
    pallas_call x1, Pallas kernels, attend(): pl.pallas_call(attend_kernel, out_shape=jax.ShapeDtypeStruct(queries.shap...  5.51 us
    pallas_call x1, Pallas kernels, attach(): pl.pallas_call(functools.partial(attach_kernel, chunk.shape[0] - SUBLANES...  2.5 us
  transfers between devices with their start and end apart: 15, of which 5 were waited for; matrix products, arithmetic and copies ran while one was open for 0% of the time, Pallas kernels for 25%

profile of v2, /device:TPU:0, one launch (start us, length us, event | category | flops | bytes accessed | tf_op | source)
XLA Modules:
  0.0 95.2 jit_solution(10934305320707448736)
XLA Ops:
  1.3 93.7 %conditional.1 = (bf16[720,2880]{1,0:T(8,128)(2,1)}, f32[1,720,90]{1,0,2:T(1,128)}, f32[1]{0:T(128)}, bf16[4,1024]{1,0:T(4,128)(2,1)}) conditional(s32[]{:T(128)} %bitcast.7, (bf16[720,2880]{1,0:T(8,128)(2,1)}, s32[90,1,720]{2,1,0:T(1,128)}, s32[4]{0:T(128)}, bf16[4,1024]{1,0:T(4,128)(2,1)}, bf16[4,2048,128]{2,1,0:T(8,128)(2,1)}, ...), branch_computations={%region_0.0_spmd, %region_1.0_spmd, %region_2.3_spmd} | conditional | flops 18 | bytes 61159052 | solution.py:462
  1.5 0.0 copy-start.6
  1.5 0.0 copy-start.11
  1.6 4.6 %dequantize_second.5 = (bf16[3344,128]{1,0:T(8,128)(2,1)}, f32[1]{0:T(128)}) custom-call(bf16[720,2880]{1,0:T(8,128)(2,1)} %get-tuple-element.74.mant_hbm.source_hbm, s32[90,1,720]{2,1,0:T(1,128)} %get-tuple-element.75.expo_ref, f32[1]{0:T(128)} %constant.37.clone.before_ref), custom_call_target="tpu_custom_call" | custom-call | tf_op jit(solution)/shard_map/cond/branch_2_fun/dequantize_second/pallas_call | solution.py:174
  6.2 1.6 %collective-permute-start.27 = (bf16[3344,128]{1,0:T(8,128)(2,1)}, bf16[3344,128]{1,0:T(8,128)(2,1)}, u32[]{:S(2)}, u32[]{:S(2)}) collective-permute-start(bf16[3344,128]{1,0:T(8,128)(2,1)} %get-tuple-element.82), channel_id=1, source_target_pairs={{8,28},{24,12},{9,29},{25,13},{10,30},{26,14},{11,31},{27,15}} | collective-permute-start | bytes 2568200 | tf_op jit(solution)/shard_map/cond/branch_2_fun/ppermute | solution.py:388
  7.8 0.0 copy-done.6
  7.8 0.0 copy-done.11
  7.8 8.0 %dequantize_rest.5 = (bf16[2880,128]{1,0:T(8,128)(2,1)}, bf16[2880,128]{1,0:T(8,128)(2,1)S(1)}, bf16[1440,128]{1,0:T(8,128)(2,1)S(1)}, bf16[3264,128]{1,0:T(8,128)(2,1)S(1)}, f32[1]{0:T(128)}) custom-call(bf16[720,2880]{1,0:T(8,128)(2,1)S(1)} %copy-done.6, s32[90,1,720]{2,1,0:T(1,128)S(1)} %copy-done.11, f32[1]{0:T(128)} %get-tuple-element.76.before_ref), custom_call_target="tpu_custom_call" | custom-call | tf_op jit(solution)/shard_map/cond/branch_2_fun/dequantize_rest/pallas_call | solution.py:174
  15.8 0.0 copy-start.2
  15.8 0.0 copy-start.3
  15.8 0.0 copy-start.14
  15.8 0.0 copy-start.17
  15.8 0.8 collective-permute-start.15
  16.7 1.2 %take.5 = bf16[2528,128]{1,0:T(8,128)(2,1)} custom-call(bf16[720,2880]{1,0:T(8,128)(2,1)S(1)} %copy-done.6), custom_call_target="tpu_custom_call" | custom-call | tf_op jit(solution)/shard_map/cond/branch_2_fun/take/pallas_call | solution.py:103
  17.8 2.8 %collective-permute-start.25 = (bf16[2528,128]{1,0:T(8,128)(2,1)}, bf16[2528,128]{1,0:T(8,128)(2,1)S(1)}, u32[]{:S(2)}, u32[]{:S(2)}) collective-permute-start(bf16[2528,128]{1,0:T(8,128)(2,1)} %take.5), channel_id=1, source_target_pairs={{0,12},{4,16},{8,20},{12,24},{16,28},{20,0},{24,4},{28,8},{1,13},{... | collective-permute-start | bytes 1941512 | tf_op jit(solution)/shard_map/cond/branch_2_fun/ppermute | solution.py:388
  20.6 1.6 %collective-permute-start.17 = (f32[1]{0:T(128)}, f32[1]{0:T(128)}, u32[]{:S(2)}, u32[]{:S(2)}) collective-permute-start(f32[1]{0:T(128)} %get-tuple-element.78.refs_0_), channel_id=1, source_target_pairs={{0,1},{1,2},{2,3},{3,0},{4,5},{5,6},{6,7},{7,4},{8,9},{9,10},{10,1... | collective-permute-start | bytes 20 | tf_op jit(solution)/shard_map/cond/branch_2_fun/ppermute | solution.py:388
  22.2 2.6 %collective-permute-start.18 = (f32[1]{0:T(128)}, f32[1]{0:T(128)}, u32[]{:S(2)}, u32[]{:S(2)}) collective-permute-start(f32[1]{0:T(128)} %get-tuple-element.78.refs_0_), channel_id=1, source_target_pairs={{0,2},{1,3},{2,0},{3,1},{4,6},{5,7},{6,4},{7,5},{8,10},{9,11},{10,... | collective-permute-start | bytes 20 | tf_op jit(solution)/shard_map/cond/branch_2_fun/ppermute | solution.py:388
  24.8 1.4 %collective-permute-done.17.refs_1_ = f32[1]{0:T(128)} collective-permute-done((f32[1]{0:T(128)}, f32[1]{0:T(128)}, u32[]{:S(2)}, u32[]{:S(2)}) %collective-permute-start.17) | collective-permute-done | bytes 36 | tf_op jit(solution)/shard_map/cond/branch_2_fun/ppermute | solution.py:388
  26.2 1.5 %collective-permute-start.23 = (bf16[2880,128]{1,0:T(8,128)(2,1)}, bf16[2880,128]{1,0:T(8,128)(2,1)}, u32[]{:S(2)}, u32[]{:S(2)}) collective-permute-start(bf16[2880,128]{1,0:T(8,128)(2,1)} %get-tuple-element.81), channel_id=1, source_target_pairs={{8,28},{24,12},{9,29},{25,13},{10,30},{26,14},{11,31},{27,15}} | collective-permute-start | bytes 2211848 | tf_op jit(solution)/shard_map/cond/branch_2_fun/ppermute | solution.py:388
  27.7 0.0 collective-permute-done.18.refs_2_
  27.7 1.8 %collective-permute-start.19 = (f32[1]{0:T(128)}, f32[1]{0:T(128)}, u32[]{:S(2)}, u32[]{:S(2)}) collective-permute-start(f32[1]{0:T(128)} %get-tuple-element.78.refs_0_), channel_id=1, source_target_pairs={{0,3},{1,0},{2,1},{3,2},{4,7},{5,4},{6,5},{7,6},{8,11},{9,8},{10,9... | collective-permute-start | bytes 20 | tf_op jit(solution)/shard_map/cond/branch_2_fun/ppermute | solution.py:388
  29.5 2.0 %collective-permute-done.19.refs_3_ = f32[1]{0:T(128)} collective-permute-done((f32[1]{0:T(128)}, f32[1]{0:T(128)}, u32[]{:S(2)}, u32[]{:S(2)}) %collective-permute-start.19) | collective-permute-done | bytes 36 | tf_op jit(solution)/shard_map/cond/branch_2_fun/ppermute | solution.py:388
  31.5 2.8 %collective-permute-start.22 = (bf16[2880,128]{1,0:T(8,128)(2,1)}, bf16[2880,128]{1,0:T(8,128)(2,1)}, u32[]{:S(2)}, u32[]{:S(2)}) collective-permute-start(bf16[2880,128]{1,0:T(8,128)(2,1)} %get-tuple-element.81), channel_id=1, source_target_pairs={{0,12},{4,16},{12,24},{16,28},{20,0},{28,8},{1,13},{5,17},{13,25},... | collective-permute-start | bytes 2211848 | tf_op jit(solution)/shard_map/cond/branch_2_fun/ppermute | solution.py:388
  34.4 0.0 collective-permute-done.15
  34.4 0.0 copy-start.18
  34.4 6.0 %collective-permute-start.26 = (bf16[3344,128]{1,0:T(8,128)(2,1)}, bf16[3344,128]{1,0:T(8,128)(2,1)S(1)}, u32[]{:S(2)}, u32[]{:S(2)}) collective-permute-start(bf16[3344,128]{1,0:T(8,128)(2,1)} %get-tuple-element.82), channel_id=1, source_target_pairs={{0,12},{4,16},{12,24},{16,28},{20,0},{28,8},{1,13},{5,17},{13,25},... | collective-permute-start | bytes 2568200 | tf_op jit(solution)/shard_map/cond/branch_2_fun/ppermute | solution.py:388
  40.4 0.0 copy-done.2
  40.5 0.0 collective-permute-done.27
  40.5 0.0 copy-done.3
  40.5 0.7 collective-permute-start.28
  41.2 0.0 copy-done.18
  41.2 2.5 %attach.5 = bf16[3264,128]{1,0:T(8,128)(2,1)S(1)} custom-call(s32[1]{0:T(128)} %bitcast.4.me_ref, f32[1]{0:T(128)} %get-tuple-element.78.refs_0_, f32[1]{0:T(128)} %collective-permute-done.17.refs_1_, f32[1]{0:T(128)} %collective-permute-done.18.refs_2_, f32[1]{0:T(128)} %collective-permute-done.19.refs_3_, ...), custom_call_target="tpu_custom_call", output_to_operand_aliasing={{}: (5, {})} | custom-call | tf_op jit(solution)/shard_map/cond/branch_2_fun/attach/pallas_call | solution.py:216
  43.7 0.0 collective-permute-done.25.refs_0_
  43.7 0.0 copy-start
  43.7 0.8 copy-done
  44.6 0.6 collective-permute-start.20
  45.2 0.0 collective-permute-done.23
  45.2 1.6 %collective-permute-start.24 = (bf16[2880,128]{1,0:T(8,128)(2,1)}, bf16[2880,128]{1,0:T(8,128)(2,1)}, u32[]{:S(2)}, u32[]{:S(2)}) collective-permute-start(bf16[2880,128]{1,0:T(8,128)(2,1)} %collective-permute-done.23), channel_id=1, source_target_pairs={{28,20},{12,4},{29,21},{13,5},{30,22},{14,6},{31,23},{15,7}} | collective-permute-start | bytes 2211848 | tf_op jit(solution)/shard_map/cond/branch_2_fun/ppermute | solution.py:388
  46.8 0.0 collective-permute-done.22.refs_0_
  46.8 3.6 %collective-permute-start.21 = (bf16[2880,128]{1,0:T(8,128)(2,1)}, bf16[2880,128]{1,0:T(8,128)(2,1)}, u32[]{:S(2)}, u32[]{:S(2)}) collective-permute-start(bf16[2880,128]{1,0:T(8,128)(2,1)} %copy-done.2), channel_id=1, source_target_pairs={{0,12},{4,16},{8,20},{12,24},{16,28},{20,0},{24,4},{28,8},{1,13},{... | collective-permute-start | bytes 2211848 | tf_op jit(solution)/shard_map/cond/branch_2_fun/ppermute | solution.py:388
  50.4 10.2 %collective-permute-done.26.refs_1_ = bf16[3344,128]{1,0:T(8,128)(2,1)S(1)} collective-permute-done((bf16[3344,128]{1,0:T(8,128)(2,1)}, bf16[3344,128]{1,0:T(8,128)(2,1)S(1)}, u32[]{:S(2)}, u32[]{:S(2)}) %collective-permute-start.26) | collective-permute-done | bytes 856096 | tf_op jit(solution)/shard_map/cond/branch_2_fun/ppermute | solution.py:388
  60.6 1.9 %collective-permute-start.14 = (bf16[1440,128]{1,0:T(8,128)(2,1)}, bf16[1440,128]{1,0:T(8,128)(2,1)}, u32[]{:S(2)}, u32[]{:S(2)}) collective-permute-start(bf16[1440,128]{1,0:T(8,128)(2,1)} %copy-done.3), channel_id=1, source_target_pairs={{0,12},{4,16},{12,24},{16,28},{20,0},{28,8},{1,13},{5,17},{13,25},... | collective-permute-start | bytes 1105928 | tf_op jit(solution)/shard_map/cond/branch_2_fun/ppermute | solution.py:388
  62.5 0.0 collective-permute-done.28.refs_2_
  62.5 1.4 %collective-permute-start.16 = (bf16[1440,128]{1,0:T(8,128)(2,1)}, bf16[1440,128]{1,0:T(8,128)(2,1)}, u32[]{:S(2)}, u32[]{:S(2)}) collective-permute-start(bf16[1440,128]{1,0:T(8,128)(2,1)} %copy-done.18), channel_id=1, source_target_pairs={{28,20},{12,4},{29,21},{13,5},{30,22},{14,6},{31,23},{15,7}} | collective-permute-start | bytes 1105928 | tf_op jit(solution)/shard_map/cond/branch_2_fun/ppermute | solution.py:388
  63.9 0.0 copy-start.1
  63.9 0.0 copy-done.14
  63.9 0.0 copy-done.17
  63.9 5.5 %attend.5.refs_6_ = bf16[4,1024]{1,0:T(4,128)(2,1)} custom-call(s32[4]{0:T(128)S(1)} %copy-done.17, bf16[4,1024]{1,0:T(4,128)(2,1)S(1)} %copy-done.14, bf16[4,2048,128]{2,1,0:T(8,128)(2,1)} %get-tuple-element.91.keys_hbm, bf16[4,2048,128]{2,1,0:T(8,128)(2,1)} %get-tuple-element.92.values_hbm), custom_call_target="tpu_custom_call" | custom-call | tf_op jit(solution)/shard_map/cond/branch_2_fun/attend/pallas_call | solution.py:370
  69.5 0.0 copy-done.1
  69.5 2.4 %branch_2_fun.4 = (bf16[720,2880]{1,0:T(8,128)(2,1)}, f32[90,1,720]{2,1,0:T(1,128)}) custom-call(bf16[2528,128]{1,0:T(8,128)(2,1)S(1)} %copy-done.1, bf16[3344,128]{1,0:T(8,128)(2,1)S(1)} %collective-permute-done.26.refs_1_, bf16[3344,128]{1,0:T(8,128)(2,1)S(1)} %collective-permute-done.28.refs_2_, s32[1]{0:T(128)} %bitcast.5.refs_3_.refs_2_), custom_call_target="tpu_custom_call" | custom-call | tf_op jit(solution)/shard_map/cond/branch_2_fun/pallas_call | solution.py:308
  71.9 0.0 collective-permute-done.24.refs_1_
  71.9 2.2 %branch_2_fun.5 = (bf16[720,2880]{1,0:T(8,128)(2,1)}, f32[90,1,720]{2,1,0:T(1,128)}) custom-call(bf16[2880,128]{1,0:T(8,128)(2,1)} %collective-permute-done.22.refs_0_, bf16[2880,128]{1,0:T(8,128)(2,1)} %collective-permute-done.24.refs_1_, s32[1]{0:T(128)} %bitcast.5.refs_3_.refs_2_, ...), custom_call_target="tpu_custom_call", output_to_operand_aliasing={{0}: (3, {}), {1}: (4, {})} | custom-call | tf_op jit(solution)/shard_map/cond/branch_2_fun/pallas_call | solution.py:308
  74.1 13.4 %collective-permute-done.21.refs_0_ = bf16[2880,128]{1,0:T(8,128)(2,1)} collective-permute-done((bf16[2880,128]{1,0:T(8,128)(2,1)}, bf16[2880,128]{1,0:T(8,128)(2,1)}, u32[]{:S(2)}, u32[]{:S(2)}) %collective-permute-start.21) | collective-permute-done | bytes 737312 | tf_op jit(solution)/shard_map/cond/branch_2_fun/ppermute | solution.py:388
  87.5 2.2 %branch_2_fun.6 = (bf16[720,2880]{1,0:T(8,128)(2,1)}, f32[90,1,720]{2,1,0:T(1,128)}) custom-call(bf16[2880,128]{1,0:T(8,128)(2,1)} %collective-permute-done.21.refs_0_, bf16[720,2880]{1,0:T(8,128)(2,1)} %get-tuple-element.85.refs_1_, f32[90,1,720]{2,1,0:T(1,128)} %get-tuple-element.86.refs_2_), custom_call_target="tpu_custom_call", output_to_operand_aliasing={{0}: (1, {}), {1}: (2, {})} | custom-call | tf_op jit(solution)/shard_map/cond/branch_2_fun/pallas_call | solution.py:308
  89.7 1.7 %collective-permute-done.14.refs_0_ = bf16[1440,128]{1,0:T(8,128)(2,1)} collective-permute-done((bf16[1440,128]{1,0:T(8,128)(2,1)}, bf16[1440,128]{1,0:T(8,128)(2,1)}, u32[]{:S(2)}, u32[]{:S(2)}) %collective-permute-start.14) | collective-permute-done | bytes 368672 | tf_op jit(solution)/shard_map/cond/branch_2_fun/ppermute | solution.py:388
  91.4 0.0 collective-permute-done.16.refs_1_
  91.5 0.0 collective-permute-done.20.refs_2_
  91.5 3.2 %branch_2_fun.7 = (bf16[720,2880]{1,0:T(8,128)(2,1)}, f32[90,1,720]{2,1,0:T(1,128)}, f32[1]{0:T(128)}, bf16[4,1024]{1,0:T(4,128)(2,1)}) custom-call(bf16[1440,128]{1,0:T(8,128)(2,1)} %collective-permute-done.14.refs_0_, bf16[1440,128]{1,0:T(8,128)(2,1)} %collective-permute-done.16.refs_1_, ...), custom_call_target="tpu_custom_call", output_to_operand_aliasing={{0}: (4, {}), {1}: (5, {}), {3}: (6, {})} | custom-call | tf_op jit(solution)/shard_map/cond/branch_2_fun/pallas_call | solution.py:308
Async XLA Ops:
  1.5 6.3 %copy-start.6 = (bf16[720,2880]{1,0:T(8,128)(2,1)S(1)}, bf16[720,2880]{1,0:T(8,128)(2,1)}, u32[]{:S(2)}) copy-start(bf16[720,2880]{1,0:T(8,128)(2,1)} %get-tuple-element.74.mant_hbm.source_hbm) | copy-start | bytes 12441604 | tf_op jit(solution)/shard_map/cond
  1.5 6.3 %copy-start.11 = (s32[90,1,720]{2,1,0:T(1,128)S(1)}, s32[90,1,720]{2,1,0:T(1,128)}, u32[]{:S(2)}) copy-start(s32[90,1,720]{2,1,0:T(1,128)} %get-tuple-element.75.expo_ref) | copy-start | bytes 777604 | tf_op jit(solution)/shard_map/cond
  6.2 34.2 %collective-permute-start.27 = (bf16[3344,128]{1,0:T(8,128)(2,1)}, bf16[3344,128]{1,0:T(8,128)(2,1)}, u32[]{:S(2)}, u32[]{:S(2)}) collective-permute-start(bf16[3344,128]{1,0:T(8,128)(2,1)} %get-tuple-element.82), channel_id=1, source_target_pairs={{8,28},{24,12},{9,29},{25,13},{10,30},{26,14},{11,31},{27,15}} | collective-permute-start | bytes 2568200 | tf_op jit(solution)/shard_map/cond/branch_2_fun/ppermute | solution.py:388
  15.8 24.6 %copy-start.2 = (bf16[2880,128]{1,0:T(8,128)(2,1)}, bf16[2880,128]{1,0:T(8,128)(2,1)S(1)}, u32[]{:S(2)}) copy-start(bf16[2880,128]{1,0:T(8,128)(2,1)S(1)} %get-tuple-element.80) | copy-start | bytes 2211844 | tf_op jit(solution)/shard_map/cond
  15.8 24.7 %copy-start.3 = (bf16[1440,128]{1,0:T(8,128)(2,1)}, bf16[1440,128]{1,0:T(8,128)(2,1)S(1)}, u32[]{:S(2)}) copy-start(bf16[1440,128]{1,0:T(8,128)(2,1)S(1)} %get-tuple-element.77) | copy-start | bytes 1105924 | tf_op jit(solution)/shard_map/cond
  15.8 48.1 %copy-start.14 = (bf16[4,1024]{1,0:T(4,128)(2,1)S(1)}, bf16[4,1024]{1,0:T(4,128)(2,1)}, u32[]{:S(2)}) copy-start(bf16[4,1024]{1,0:T(4,128)(2,1)} %get-tuple-element.90.queries_ref) | copy-start | bytes 24580 | tf_op jit(solution)/shard_map/cond
  15.8 48.1 %copy-start.17 = (s32[4]{0:T(128)S(1)}, s32[4]{0:T(128)}, u32[]{:S(2)}) copy-start(s32[4]{0:T(128)} %get-tuple-element.89.lengths_ref) | copy-start | bytes 52 | tf_op jit(solution)/shard_map/cond
  15.8 18.5 %collective-permute-start.15 = (bf16[1440,128]{1,0:T(8,128)(2,1)S(1)}, bf16[1440,128]{1,0:T(8,128)(2,1)S(1)}, u32[]{:S(2)}, u32[]{:S(2)}) collective-permute-start(bf16[1440,128]{1,0:T(8,128)(2,1)S(1)} %get-tuple-element.77), channel_id=1, source_target_pairs={{8,28},{24,12},{9,29},{25,13},{10,30},{26,14},{11,31},{27,15}} | collective-permute-start | bytes 1105928 | tf_op jit(solution)/shard_map/cond/branch_2_fun/ppermute | solution.py:388
  17.8 25.9 %collective-permute-start.25 = (bf16[2528,128]{1,0:T(8,128)(2,1)}, bf16[2528,128]{1,0:T(8,128)(2,1)S(1)}, u32[]{:S(2)}, u32[]{:S(2)}) collective-permute-start(bf16[2528,128]{1,0:T(8,128)(2,1)} %take.5), channel_id=1, source_target_pairs={{0,12},{4,16},{8,20},{12,24},{16,28},{20,0},{24,4},{28,8},{1,13},{... | collective-permute-start | bytes 1941512 | tf_op jit(solution)/shard_map/cond/branch_2_fun/ppermute | solution.py:388
  20.6 5.6 %collective-permute-start.17 = (f32[1]{0:T(128)}, f32[1]{0:T(128)}, u32[]{:S(2)}, u32[]{:S(2)}) collective-permute-start(f32[1]{0:T(128)} %get-tuple-element.78.refs_0_), channel_id=1, source_target_pairs={{0,1},{1,2},{2,3},{3,0},{4,5},{5,6},{6,7},{7,4},{8,9},{9,10},{10,1... | collective-permute-start | bytes 20 | tf_op jit(solution)/shard_map/cond/branch_2_fun/ppermute | solution.py:388
  22.2 5.5 %collective-permute-start.18 = (f32[1]{0:T(128)}, f32[1]{0:T(128)}, u32[]{:S(2)}, u32[]{:S(2)}) collective-permute-start(f32[1]{0:T(128)} %get-tuple-element.78.refs_0_), channel_id=1, source_target_pairs={{0,2},{1,3},{2,0},{3,1},{4,6},{5,7},{6,4},{7,5},{8,10},{9,11},{10,... | collective-permute-start | bytes 20 | tf_op jit(solution)/shard_map/cond/branch_2_fun/ppermute | solution.py:388
  26.2 19.0 %collective-permute-start.23 = (bf16[2880,128]{1,0:T(8,128)(2,1)}, bf16[2880,128]{1,0:T(8,128)(2,1)}, u32[]{:S(2)}, u32[]{:S(2)}) collective-permute-start(bf16[2880,128]{1,0:T(8,128)(2,1)} %get-tuple-element.81), channel_id=1, source_target_pairs={{8,28},{24,12},{9,29},{25,13},{10,30},{26,14},{11,31},{27,15}} | collective-permute-start | bytes 2211848 | tf_op jit(solution)/shard_map/cond/branch_2_fun/ppermute | solution.py:388
  27.7 3.8 %collective-permute-start.19 = (f32[1]{0:T(128)}, f32[1]{0:T(128)}, u32[]{:S(2)}, u32[]{:S(2)}) collective-permute-start(f32[1]{0:T(128)} %get-tuple-element.78.refs_0_), channel_id=1, source_target_pairs={{0,3},{1,0},{2,1},{3,2},{4,7},{5,4},{6,5},{7,6},{8,11},{9,8},{10,9... | collective-permute-start | bytes 20 | tf_op jit(solution)/shard_map/cond/branch_2_fun/ppermute | solution.py:388
  31.5 15.3 %collective-permute-start.22 = (bf16[2880,128]{1,0:T(8,128)(2,1)}, bf16[2880,128]{1,0:T(8,128)(2,1)}, u32[]{:S(2)}, u32[]{:S(2)}) collective-permute-start(bf16[2880,128]{1,0:T(8,128)(2,1)} %get-tuple-element.81), channel_id=1, source_target_pairs={{0,12},{4,16},{12,24},{16,28},{20,0},{28,8},{1,13},{5,17},{13,25},... | collective-permute-start | bytes 2211848 | tf_op jit(solution)/shard_map/cond/branch_2_fun/ppermute | solution.py:388
  34.4 6.8 %copy-start.18 = (bf16[1440,128]{1,0:T(8,128)(2,1)}, bf16[1440,128]{1,0:T(8,128)(2,1)S(1)}, u32[]{:S(2)}) copy-start(bf16[1440,128]{1,0:T(8,128)(2,1)S(1)} %collective-permute-done.15) | copy-start | bytes 1105924 | tf_op jit(solution)/shard_map/cond
  34.4 26.2 %collective-permute-start.26 = (bf16[3344,128]{1,0:T(8,128)(2,1)}, bf16[3344,128]{1,0:T(8,128)(2,1)S(1)}, u32[]{:S(2)}, u32[]{:S(2)}) collective-permute-start(bf16[3344,128]{1,0:T(8,128)(2,1)} %get-tuple-element.82), channel_id=1, source_target_pairs={{0,12},{4,16},{12,24},{16,28},{20,0},{28,8},{1,13},{5,17},{13,25},... | collective-permute-start | bytes 2568200 | tf_op jit(solution)/shard_map/cond/branch_2_fun/ppermute | solution.py:388
  40.5 22.0 %collective-permute-start.28 = (bf16[3344,128]{1,0:T(8,128)(2,1)}, bf16[3344,128]{1,0:T(8,128)(2,1)S(1)}, u32[]{:S(2)}, u32[]{:S(2)}) collective-permute-start(bf16[3344,128]{1,0:T(8,128)(2,1)} %collective-permute-done.27), channel_id=1, source_target_pairs={{28,20},{12,4},{29,21},{13,5},{30,22},{14,6},{31,23},{15,7}} | collective-permute-start | bytes 2568200 | tf_op jit(solution)/shard_map/cond/branch_2_fun/ppermute | solution.py:388
  43.7 0.8 copy-start
  44.6 46.9 %collective-permute-start.20 = (bf16[3264,128]{1,0:T(8,128)(2,1)S(1)}, bf16[3264,128]{1,0:T(8,128)(2,1)S(1)}, u32[]{:S(2)}, u32[]{:S(2)}) collective-permute-start(bf16[3264,128]{1,0:T(8,128)(2,1)S(1)} %attach.5), channel_id=1, source_target_pairs={{0,12},{4,16},{8,20},{12,24},{16,28},{20,0},{24,4},{28,8},{1,13},{... | collective-permute-start | bytes 2506760 | tf_op jit(solution)/shard_map/cond/branch_2_fun/ppermute | solution.py:388
  45.2 26.7 %collective-permute-start.24 = (bf16[2880,128]{1,0:T(8,128)(2,1)}, bf16[2880,128]{1,0:T(8,128)(2,1)}, u32[]{:S(2)}, u32[]{:S(2)}) collective-permute-start(bf16[2880,128]{1,0:T(8,128)(2,1)} %collective-permute-done.23), channel_id=1, source_target_pairs={{28,20},{12,4},{29,21},{13,5},{30,22},{14,6},{31,23},{15,7}} | collective-permute-start | bytes 2211848 | tf_op jit(solution)/shard_map/cond/branch_2_fun/ppermute | solution.py:388
  46.8 40.7 %collective-permute-start.21 = (bf16[2880,128]{1,0:T(8,128)(2,1)}, bf16[2880,128]{1,0:T(8,128)(2,1)}, u32[]{:S(2)}, u32[]{:S(2)}) collective-permute-start(bf16[2880,128]{1,0:T(8,128)(2,1)} %copy-done.2), channel_id=1, source_target_pairs={{0,12},{4,16},{8,20},{12,24},{16,28},{20,0},{24,4},{28,8},{1,13},{... | collective-permute-start | bytes 2211848 | tf_op jit(solution)/shard_map/cond/branch_2_fun/ppermute | solution.py:388
  60.6 30.9 %collective-permute-start.14 = (bf16[1440,128]{1,0:T(8,128)(2,1)}, bf16[1440,128]{1,0:T(8,128)(2,1)}, u32[]{:S(2)}, u32[]{:S(2)}) collective-permute-start(bf16[1440,128]{1,0:T(8,128)(2,1)} %copy-done.3), channel_id=1, source_target_pairs={{0,12},{4,16},{12,24},{16,28},{20,0},{28,8},{1,13},{5,17},{13,25},... | collective-permute-start | bytes 1105928 | tf_op jit(solution)/shard_map/cond/branch_2_fun/ppermute | solution.py:388
  62.5 28.9 %collective-permute-start.16 = (bf16[1440,128]{1,0:T(8,128)(2,1)}, bf16[1440,128]{1,0:T(8,128)(2,1)}, u32[]{:S(2)}, u32[]{:S(2)}) collective-permute-start(bf16[1440,128]{1,0:T(8,128)(2,1)} %copy-done.18), channel_id=1, source_target_pairs={{28,20},{12,4},{29,21},{13,5},{30,22},{14,6},{31,23},{15,7}} | collective-permute-start | bytes 1105928 | tf_op jit(solution)/shard_map/cond/branch_2_fun/ppermute | solution.py:388
  63.9 5.5 %copy-start.1 = (bf16[2528,128]{1,0:T(8,128)(2,1)S(1)}, bf16[2528,128]{1,0:T(8,128)(2,1)}, u32[]{:S(2)}) copy-start(bf16[2528,128]{1,0:T(8,128)(2,1)} %copy-done) | copy-start | bytes 1941508 | tf_op jit(solution)/shard_map/cond
